TPU v7x, 32 devices: a whole 2x2x4 slice. The times are simulated.
32 devices in a mesh: shard: 8 (over z, x), tp: 4 (over y, core).
Axes of the slice: x: 2, y: 2, z: 4, core: 2. Of those that a mesh axis runs over, the one named last changes fastest.
Arguments:
- one_gate: float32 [2048, 8192], P('shard', 'tp'), may hold values from -0.1875 to 0.1875
- other_gate: float32 [2048, 8192], P('shard', 'tp'), may hold values from -0.125 to 0.125
- one_up: float32 [2048, 8192], P('shard', 'tp'), may hold values from -0.1875 to 0.1875
- other_up: float32 [2048, 8192], P('shard', 'tp'), may hold values from -0.125 to 0.125
- mix_share: float32 [2048], P('shard'), may hold values from 0.2 to 0.8
- norm_train: float32 [2048], P(('shard', 'tp')), may hold values from 0.25 to 1.75
- norm_step: float32 [2048], P(('shard', 'tp')), may hold values from -0.3 to 0.3
Outputs:
- serve_gate: bfloat16 [2048, 8192], P(None, 'tp')
- serve_up: bfloat16 [2048, 8192], P(None, 'tp')
- factor_gate: float32 [8192], P('tp')
- factor_up: float32 [8192], P('tp')
- serve_norm: bfloat16 [2048], replicated
All inputs are finite; a program needn't handle non-finite values.
Results may differ from a plain program's by a relative error of at most 0.0004.
Values may be sent and summed in bfloat16 or wider, within the bound.
A program may use at most 128 MiB of HBM per device.

v0:
```python
import functools

import jax
import jax.numpy as jnp
from jax import lax
from jax.experimental import pallas as pl
from jax.experimental.pallas import tpu as pltpu
from jax.sharding import PartitionSpec as P

MESH = pl.DeviceIdType.MESH
UP, DOWN, ACROSS = 0, 1, 2


def gather_kernel(
    n, parts, pieces, one_gate, other_gate, one_up, other_up, mix, train, step,
    held, factor_gate, factor_up, norm,
    ones, others, sums, mix_row, shares, gains, in_sem, small_sem,
    sum_send, sum_recv, norm_send, norm_recv, send_sem, recv_sem,
):
    me = lax.axis_index("shard")
    part = lax.axis_index("tp")
    m, half = n // 2, pieces // 2
    place, side = me // 2, me % 2
    rows, cols = ones.shape[1:]
    tall = rows // half
    lanes = shares.shape[1]

    barrier = pltpu.get_barrier_semaphore()

    @pl.loop(1, n)
    def _(off):
        pl.semaphore_signal(barrier, inc=1, device_id={"shard": lax.rem(me + off, n)}, device_id_type=MESH)

    @pl.loop(1, parts)
    def _(off):
        pl.semaphore_signal(barrier, inc=1, device_id={"tp": lax.rem(part + off, parts)}, device_id_type=MESH)

    read_mix = pltpu.make_async_copy(mix, mix_row, small_sem.at[0])
    read_gains = [
        pltpu.make_async_copy(source, gains.at[i], small_sem.at[1 + i]) for i, source in enumerate((train, step))
    ]

    def reads(piece):
        a, at = piece // half, pl.ds(piece % half * tall, tall)
        first, second = ((one_gate, other_gate), (one_up, other_up))[a]
        return (
            pltpu.make_async_copy(first.at[at], ones.at[a, at], in_sem.at[0, piece]),
            pltpu.make_async_copy(second.at[at], others.at[a, at], in_sem.at[1, piece]),
        )

    read_mix.start()
    for piece in range(half):
        for copy in reads(piece):
            copy.start()
    read_mix.wait()
    shares[...] = jnp.transpose(jnp.broadcast_to(mix_row[...], (lanes, shares.shape[0])))

    def mix_and_sum(a):
        total = jnp.zeros((8, cols), jnp.float32)
        for piece in range(a * half, (a + 1) * half):
            for copy in reads(piece):
                copy.wait()

            def mixed(r, total):
                at = pl.ds(pl.multiple_of(piece % half * tall + r * 8, 8), 8)
                share = shares[at]
                rest = 1.0 - share
                share, rest = (jnp.concatenate([v] * (cols // lanes), axis=1) for v in (share, rest))
                fresh = share * ones[a, at] + rest * others[a, at]
                ones[a, at] = fresh
                return total + fresh * fresh

            total = lax.fori_loop(0, tall // 8, mixed, total, unroll=4)
        sums[a, me] = jnp.sum(total, axis=0, keepdims=True)

    def sum_copy(a, off):
        return pltpu.make_async_remote_copy(
            src_ref=sums.at[a, me], dst_ref=sums.at[a, me],
            send_sem=sum_send.at[a, off], recv_sem=sum_recv.at[a, off],
            device_id={"shard": lax.rem(me + off, n)}, device_id_type=MESH,
        )

    def exchange(a):
        @pl.loop(1, n)
        def _(off):
            sum_copy(a, off).start()

    def scales(a):
        @pl.loop(1, n)
        def _(off):
            sum_copy(a, off).wait_recv()

        factors = jnp.sqrt(lax.fori_loop(1, n, lambda i, t: t + sums[a, i], sums[a, 0]))
        (factor_gate, factor_up)[a][...] = factors
        return jnp.broadcast_to(1.0 / factors, (8, cols))

    def norm_row(off):
        return pltpu.make_async_remote_copy(
            src_ref=norm.at[me, part], dst_ref=norm.at[me, part],
            send_sem=norm_send.at[off], recv_sem=norm_recv.at[off],
            device_id={"tp": lax.rem(part + off, parts)}, device_id_type=MESH,
        )

    def norm_group(off):
        return pltpu.make_async_remote_copy(
            src_ref=norm.at[me], dst_ref=norm.at[me],
            send_sem=norm_send.at[parts + off], recv_sem=norm_recv.at[parts + off],
            device_id={"shard": lax.rem(me + off, n)}, device_id_type=MESH,
        )

    def piece_of(j, s, c):
        at = pl.multiple_of((2 * j + s) * rows + c % half * tall, 8)
        return held.at[c // half, pl.ds(at, tall)]

    def send(way, j, s, c, slot=None):
        target = {
            UP: {"shard": lax.rem(me + 2, n)},
            DOWN: {"shard": lax.rem(me + n - 2, n)},
            ACROSS: {"shard": 2 * place + 1 - side},
        }[way]
        block = piece_of(j, s, c)
        return pltpu.make_async_remote_copy(
            src_ref=block, dst_ref=block,
            send_sem=send_sem.at[way * m + j if slot is None else slot, c],
            recv_sem=recv_sem.at[2 * j + s, c],
            device_id=target, device_id_type=MESH,
        )

    def arrived(j, s, c):
        block = piece_of(j, s, c)
        pltpu.make_async_copy(block, block, recv_sem.at[2 * j + s, c]).wait()

    last = m - 1
    first_place, last_place = place == 0, place == last

    def crosses(j, c):
        kept = (first_place & (j == 1)) | (last_place & (j == last - 1))
        kept = kept & (c >= half)
        return ~(kept | ((place == 1) & (j == 0)) | ((place == last - 1) & (j == last)))

    def own(a):
        scale = scales(a)
        for c in range(a * half, (a + 1) * half):
            at = c % half * tall

            def scaled(r, _):
                here = pl.multiple_of(at + r * 8, 8)
                there = pl.multiple_of(me * rows + at + r * 8, 8)
                held[a, pl.ds(there, 8)] = (ones[a, pl.ds(here, 8)] * scale).astype(jnp.bfloat16)
                return 0

            lax.fori_loop(0, tall // 8, scaled, 0, unroll=4)

            @pl.when(~last_place)
            def _():
                send(UP, place, side, c).start()

            @pl.when(~first_place)
            def _():
                send(DOWN, place, side, c).start()

            send(ACROSS, place, side, c).start()

    mix_and_sum(0)
    pl.semaphore_wait(barrier, n + parts - 2)
    exchange(0)
    for piece in range(half, pieces):
        for copy in reads(piece):
            copy.start()
    for copy in read_gains:
        copy.start()
    own(0)
    for copy in read_gains:
        copy.wait()
    norm[me, part] = gains[0] + gains[1]

    @pl.loop(1, parts)
    def _(off):
        norm_row(off).start()

    mix_and_sum(1)
    exchange(1)

    @pl.loop(1, parts)
    def _(off):
        norm_row(off).wait()

    @pl.loop(1, n)
    def _(off):
        norm_group(off).start()

    own(1)
    extra = 3 * m

    def ends(b, c):
        return (first_place | last_place) & (b == 1)

    def inner(b, c):
        return ((place == 1) | (place == last - 1)) & (b == last - 1) & (c >= half)

    @pl.loop(0, last * pieces)
    def _(slot):
        b, c = slot // pieces, slot % pieces

        @pl.when(b < place)
        def _():
            j = place - 1 - b
            arrived(j, side, c)

            @pl.when(~last_place)
            def _():
                send(UP, j, side, c).start()

            @pl.when(crosses(j, c))
            def _():
                send(ACROSS, j, side, c).start()

        @pl.when(b < last - place)
        def _():
            j = place + 1 + b
            arrived(j, side, c)

            @pl.when(~first_place)
            def _():
                send(DOWN, j, side, c).start()

            @pl.when(crosses(j, c))
            def _():
                send(ACROSS, j, side, c).start()

        @pl.when(ends(b, c) | inner(b, c))
        def _():
            arrived(place, 1 - side, c)

            @pl.when(first_place | (place == last - 1))
            def _():
                send(UP, place, 1 - side, c, extra).start()

            @pl.when(last_place | (place == 1))
            def _():
                send(DOWN, place, 1 - side, c, extra).start()

    passed_on = first_place | last_place
    passed_half = (place == 1) | (place == last - 1)
    inward = jnp.where(first_place, 1, last - 1)

    @pl.loop(1, n)
    def _(off):
        sum_copy(0, off).wait_send()
        sum_copy(1, off).wait_send()
        norm_group(off).wait()

    @pl.loop(0, m * pieces)
    def _(slot):
        b, c = slot // pieces, slot % pieces
        j = jnp.where(2 * place < last, b, last - b)
        passed = (j == place) & (passed_on | (passed_half & (c >= half)))
        late = passed_on & (j == inward) & (c >= half)

        @pl.when((j <= place) & ~last_place)
        def _():
            send(UP, j, side, c).wait_send()

        @pl.when((j >= place) & ~first_place)
        def _():
            send(DOWN, j, side, c).wait_send()

        @pl.when(passed)
        def _():
            send(UP, place, 1 - side, c, extra).wait_send()

        @pl.when(crosses(j, c))
        def _():
            send(ACROSS, j, side, c).wait_send()

        @pl.when(~(passed | late))
        def _():
            arrived(j, 1 - side, c)

    @pl.when(passed_on)
    def _():
        for c in range(half, pieces):
            arrived(inward, 1 - side, c)


def write_kernel(n, held, factor_gate, factor_up, gate, up, out_gate, out_up, sem, small_sem):
    rows = held.shape[1] // n
    copies = [
        pltpu.make_async_copy(held.at[a, pl.ds(i * rows, rows)], out.at[pl.ds(i * rows, rows)], sem.at[a, i])
        for i in range(n)
        for a, out in enumerate((gate, up))
    ]
    copies.append(pltpu.make_async_copy(factor_gate, out_gate, small_sem.at[0]))
    copies.append(pltpu.make_async_copy(factor_up, out_up, small_sem.at[1]))
    for copy in copies:
        copy.start()
    for copy in copies:
        copy.wait()


def shards(n, parts, one_gate, other_gate, one_up, other_up, mix_share, norm_train, norm_step):
    rows, cols = one_gate.shape
    few = norm_train.shape[0]
    lanes = 128
    padded = -(-rows // lanes) * lanes
    pieces = 2 * max(1, rows // 64)
    kinds = pltpu.SemaphoreType
    vmem, anywhere = pl.BlockSpec(memory_space=pltpu.VMEM), pl.BlockSpec(memory_space=pl.ANY)
    held, factor_gate, factor_up, norm = pl.pallas_call(
        functools.partial(gather_kernel, n, parts, pieces),
        out_shape=(
            pltpu.VMEM((2, n * rows, cols), jnp.bfloat16),
            pltpu.VMEM((1, cols), jnp.float32),
            pltpu.VMEM((1, cols), jnp.float32),
            pltpu.VMEM((n, parts, 1, few), jnp.float32),
        ),
        in_specs=[pl.BlockSpec(memory_space=pltpu.HBM)] * 7,
        out_specs=(vmem,) * 4,
        scratch_shapes=[
            pltpu.VMEM((2, rows, cols), jnp.float32),
            pltpu.VMEM((2, rows, cols), jnp.float32),
            pltpu.VMEM((2, n, 1, cols), jnp.float32),
            pltpu.VMEM((1, padded), jnp.float32),
            pltpu.VMEM((padded, lanes), jnp.float32),
            pltpu.VMEM((2, 1, few), jnp.float32),
            kinds.DMA((2, pieces)),
            kinds.DMA((3,)),
            kinds.DMA((2, n)),
            kinds.DMA((2, n)),
            kinds.DMA((n + parts,)),
            kinds.DMA((n + parts,)),
            kinds.DMA((3 * (n // 2) + 1, pieces)),
            kinds.DMA((n, pieces)),
        ],
        compiler_params=pltpu.CompilerParams(
            collective_id=0, has_side_effects=True, vmem_limit_bytes=46 * 2**20
        ),
        name="mix_gather",
    )(
        one_gate, other_gate, one_up, other_up,
        jnp.pad(mix_share, (0, padded - rows))[None], norm_train[None], norm_step[None],
    )
    gate, up, factor_gate, factor_up = pl.pallas_call(
        functools.partial(write_kernel, n),
        out_shape=(jax.ShapeDtypeStruct((n * rows, cols), jnp.bfloat16),) * 2
        + (jax.ShapeDtypeStruct((1, cols), jnp.float32),) * 2,
        in_specs=[vmem] * 3,
        out_specs=(anywhere,) * 4,
        scratch_shapes=[kinds.DMA((2, n)), kinds.DMA((2,))],
        compiler_params=pltpu.CompilerParams(vmem_limit_bytes=2**20),
        name="write_out",
    )(held, factor_gate, factor_up)
    return gate, up, factor_gate[0], factor_up[0], norm.reshape(-1).astype(jnp.bfloat16)


def solution(mesh):
    return jax.shard_map(
        functools.partial(shards, mesh.shape["shard"], mesh.shape["tp"]),
        mesh=mesh,
        in_specs=(
            P("shard", "tp"),
            P("shard", "tp"),
            P("shard", "tp"),
            P("shard", "tp"),
            P("shard"),
            P(("shard", "tp")),
            P(("shard", "tp")),
        ),
        out_specs=(P(None, "tp"), P(None, "tp"), P("tp"), P("tp"), P()),
        check_vma=False,
    )
```

profile of v0, /device:TPU:0, one launch (start us, length us, event | category | flops | bytes accessed | tf_op | source)
XLA Modules:
  0.0 179.4 jit_solution(7337711700212073556)
XLA Ops:
  0.6 172.0 %mix_gather.1 = (bf16[2,2048,2048]{2,1,0:T(8,128)(2,1)S(1)}, f32[1,2048]{1,0:T(1,128)S(1)}, f32[1,2048]{1,0:T(1,128)S(1)}, f32[8,4,1,64]{3,2,1,0:T(1,128)S(1)}) custom-call(f32[256,2048]{1,0:T(8,128)} %one_gate.1, f32[256,2048]{1,0:T(8,128)} %other_gate.1, f32[256,2048]{1,0:T(8,128)} %one_up.1, f32[256,2048]{1,0:T(8,128)} %other_up.1, f32[1,256]{1,0:T(1,128)} %bitcast.5, ...), custom_call_target="tpu_custom_call" | custom-call | tf_op jit(solution)/shard_map/mix_gather/pallas_call | solution.py:309
  172.7 6.0 %write_out.1 = (bf16[2048,2048]{1,0:T(8,128)(2,1)}, bf16[2048,2048]{1,0:T(8,128)(2,1)}, f32[1,2048]{1,0:T(1,128)}, f32[1,2048]{1,0:T(1,128)}) custom-call(bf16[2,2048,2048]{2,1,0:T(8,128)(2,1)S(1)} %get-tuple-element.13.held, f32[1,2048]{1,0:T(1,128)S(1)} %get-tuple-element.14.factor_gate, f32[1,2048]{1,0:T(1,128)S(1)} %get-tuple-element.15.factor_up), custom_call_target="tpu_custom_call" | custom-call | tf_op jit(solution)/shard_map/write_out/pallas_call | solution.py:343
  178.7 0.1 convert_reduce_fusion
  178.7 0.7 convert_element_type.7
where the time goes:
time: 180 us; the launch traced here: 179 us
  Pallas kernels  178 us (99%)
    pallas_call x1, Pallas kernels, shards(): pl.pallas_call(functools.partial(gather_kernel, n, parts, pieces), out_sh...  172 us
    pallas_call x1, Pallas kernels, shards(): pl.pallas_call(functools.partial(write_kernel, n), out_shape=(jax.ShapeDt...  5.99 us

commit v1 on v0

v1 whole, which is shorter than its diff:
```python
import functools

import jax
import jax.numpy as jnp
import numpy as np
from jax import lax
from jax.experimental import pallas as pl
from jax.experimental.pallas import tpu as pltpu
from jax.sharding import PartitionSpec as P

MESH = pl.DeviceIdType.MESH
UP, DOWN, ACROSS = 0, 1, 2


def crosses(place, m, pieces, j, c):
    last = m - 1
    kept = ((place == 0) & (j == 1)) | ((place == last) & (j == last - 1))
    kept = kept & (c >= pieces // 2)
    return ~(kept | ((place == 1) & (j == 0)) | ((place == last - 1) & (j == last)))


def sent(m, pieces, place):
    last, half = m - 1, pieces // 2
    extra = pieces if last > 1 and place in (0, last) else 0
    inner = pieces - half if last > 1 and place in (1, last - 1) else 0
    up = (place + 1) * pieces * (place != last) + extra * (place == 0) + inner * (place == last - 1)
    down = (m - place) * pieces * (place != 0) + extra * (place == last) + inner * (place == 1)
    across = pieces + sum(
        bool(crosses(np.int64(place), m, pieces, np.int64(j), np.int64(c)))
        for j in range(m) if j != place for c in range(pieces)
    )
    return up, down, across


def gather_kernel(
    n, parts, pieces, one_gate, other_gate, one_up, other_up, mix, train, step,
    held, factor_gate, factor_up, gain,
    ones, others, sums, mix_row, shares, gains, norm, gain_rows,
    in_sem, small_sem, sum_send, sum_recv, norm_sem, send_sem, recv_sem, rest_sem,
):
    me = lax.axis_index("shard")
    part = lax.axis_index("tp")
    m, half = n // 2, pieces // 2
    place, side = me // 2, me % 2
    rows, cols = ones.shape[1:]
    tall = rows // half
    mine = me * parts + part
    lanes = shares.shape[1]

    barrier = pltpu.get_barrier_semaphore()

    @pl.loop(1, n)
    def _(off):
        pl.semaphore_signal(barrier, inc=1, device_id={"shard": lax.rem(me + off, n)}, device_id_type=MESH)

    @pl.loop(1, parts)
    def _(off):
        pl.semaphore_signal(barrier, inc=1, device_id={"tp": lax.rem(part + off, parts)}, device_id_type=MESH)

    read_mix = pltpu.make_async_copy(mix, mix_row, small_sem.at[0])
    read_gains = [
        pltpu.make_async_copy(source, gains.at[i], small_sem.at[1]) for i, source in enumerate((train, step))
    ]

    def reads(piece):
        a, at = piece // half, pl.ds(piece % half * tall, tall)
        first, second = ((one_gate, other_gate), (one_up, other_up))[a]
        return (
            pltpu.make_async_copy(first.at[at], ones.at[a, at], in_sem.at[piece]),
            pltpu.make_async_copy(second.at[at], others.at[a, at], in_sem.at[piece]),
        )

    def took(ref, sem):
        pltpu.make_async_copy(ref, ref, sem).wait()

    read_mix.start()
    for piece in range(half):
        for copy in reads(piece):
            copy.start()
    read_mix.wait()
    shares[...] = jnp.transpose(jnp.broadcast_to(mix_row[...], (lanes, shares.shape[0])))

    def mix_and_sum(a):
        total = jnp.zeros((8, cols), jnp.float32)
        for piece in range(a * half, (a + 1) * half):
            took(ones.at[:, pl.ds(0, tall)], in_sem.at[piece])

            def mixed(r, total):
                at = pl.ds(pl.multiple_of(piece % half * tall + r * 8, 8), 8)
                share = shares[at]
                rest = 1.0 - share
                share, rest = (jnp.concatenate([v] * (cols // lanes), axis=1) for v in (share, rest))
                fresh = share * ones[a, at] + rest * others[a, at]
                ones[a, at] = fresh
                return total + fresh * fresh

            total = lax.fori_loop(0, tall // 8, mixed, total, unroll=4)
        sums[a, me] = jnp.sum(total, axis=0, keepdims=True)

    def sum_copy(a, off):
        return pltpu.make_async_remote_copy(
            src_ref=sums.at[a, me], dst_ref=sums.at[a, me],
            send_sem=sum_send.at[0], recv_sem=sum_recv.at[a],
            device_id={"shard": lax.rem(me + off, n)}, device_id_type=MESH,
        )

    def exchange(a):
        @pl.loop(1, n)
        def _(off):
            sum_copy(a, off).start()

    def scales(a):
        took(sums.at[a, pl.ds(0, n - 1)], sum_recv.at[a])
        factors = jnp.sqrt(lax.fori_loop(1, n, lambda i, t: t + sums[a, i], sums[a, 0]))
        (factor_gate, factor_up)[a][...] = factors
        return jnp.broadcast_to(1.0 / factors, (8, cols))

    def norm_row(off):
        return pltpu.make_async_remote_copy(
            src_ref=norm.at[mine], dst_ref=norm.at[mine],
            send_sem=norm_sem.at[0], recv_sem=norm_sem.at[1],
            device_id={"tp": lax.rem(part + off, parts)}, device_id_type=MESH,
        )

    def norm_group(off):
        return pltpu.make_async_remote_copy(
            src_ref=norm.at[pl.ds(me * parts, parts)], dst_ref=norm.at[pl.ds(me * parts, parts)],
            send_sem=norm_sem.at[0], recv_sem=norm_sem.at[2],
            device_id={"shard": lax.rem(me + off, n)}, device_id_type=MESH,
        )

    def piece_of(j, s, c):
        at = pl.multiple_of((c // half * n + 2 * j + s) * rows + c % half * tall, 8)
        return held.at[pl.ds(at, tall)]

    def send(way, j, s, c, rest=False):
        target = {
            UP: {"shard": lax.rem(me + 2, n)},
            DOWN: {"shard": lax.rem(me + n - 2, n)},
            ACROSS: {"shard": 2 * place + 1 - side},
        }[way]
        block = piece_of(j, s, c)
        return pltpu.make_async_remote_copy(
            src_ref=block, dst_ref=block,
            send_sem=send_sem.at[way], recv_sem=rest_sem.at[0] if rest else recv_sem.at[j, c],
            device_id=target, device_id_type=MESH,
        )

    def arrived(j, s, c):
        took(piece_of(j, s, c), recv_sem.at[j, c])

    last = m - 1
    first_place, last_place = place == 0, place == last

    def own(a):
        scale = scales(a)
        for c in range(a * half, (a + 1) * half):
            at = c % half * tall

            def scaled(r, _):
                here = pl.multiple_of(at + r * 8, 8)
                there = pl.multiple_of((a * n + me) * rows + at + r * 8, 8)
                held[pl.ds(there, 8)] = (ones[a, pl.ds(here, 8)] * scale).astype(jnp.bfloat16)
                return 0

            lax.fori_loop(0, tall // 8, scaled, 0, unroll=4)

            @pl.when(~last_place)
            def _():
                send(UP, place, side, c).start()

            @pl.when(~first_place)
            def _():
                send(DOWN, place, side, c).start()

            send(ACROSS, place, side, c).start()

    mix_and_sum(0)
    pl.semaphore_wait(barrier, n + parts - 2)
    exchange(0)
    for piece in range(half, pieces):
        for copy in reads(piece):
            copy.start()
    for copy in read_gains:
        copy.start()
    own(0)
    took(gains, small_sem.at[1])
    few = gains.shape[2]
    per = lanes // few
    lane = lax.broadcasted_iota(jnp.int32, (1, lanes), 1)
    summed = jnp.concatenate([gains[0] + gains[1]] * per, axis=1)
    norm[mine] = jnp.where(lane // few == mine % per, summed, 0.0)

    @pl.loop(1, parts)
    def _(off):
        norm_row(off).start()

    mix_and_sum(1)
    exchange(1)

    took(norm.at[pl.ds(0, parts - 1)], norm_sem.at[1])

    @pl.loop(1, n)
    def _(off):
        norm_group(off).start()

    own(1)
    took(norm.at[pl.ds(0, (n - 1) * parts)], norm_sem.at[2])

    @pl.loop(0, gain.shape[0])
    def _(r):
        gain_rows[pl.ds(r, 1)] = functools.reduce(lambda t, i: t + norm[r * per + i], range(1, per), norm[r * per])

    gain[...] = gain_rows[...].astype(jnp.bfloat16)

    def ends(b, c):
        return (first_place | last_place) & (b == 1)

    def inner(b, c):
        return ((place == 1) | (place == last - 1)) & (b == last - 1) & (c >= half)

    @pl.loop(0, last * pieces)
    def _(slot):
        b, c = slot // pieces, slot % pieces

        @pl.when(b < place)
        def _():
            j = place - 1 - b
            arrived(j, side, c)

            @pl.when(~last_place)
            def _():
                send(UP, j, side, c).start()

            @pl.when(crosses(place, m, pieces, j, c))
            def _():
                send(ACROSS, j, side, c, True).start()

        @pl.when(b < last - place)
        def _():
            j = place + 1 + b
            arrived(j, side, c)

            @pl.when(~first_place)
            def _():
                send(DOWN, j, side, c).start()

            @pl.when(crosses(place, m, pieces, j, c))
            def _():
                send(ACROSS, j, side, c, True).start()

        @pl.when(ends(b, c) | inner(b, c))
        def _():
            arrived(place, 1 - side, c)

            @pl.when(first_place | (place == last - 1))
            def _():
                send(UP, place, 1 - side, c, True).start()

            @pl.when(last_place | (place == 1))
            def _():
                send(DOWN, place, 1 - side, c, True).start()

    @pl.loop(0, pieces)
    def _(c):
        @pl.when(~(first_place | last_place | (((place == 1) | (place == last - 1)) & (c >= half))))
        def _():
            arrived(place, 1 - side, c)

    took(held.at[pl.ds(0, last * pieces * tall)], rest_sem.at[0])
    took(sums.at[:, pl.ds(0, n - 1)], sum_send.at[0])
    took(norm.at[pl.ds(0, n * parts - 1)], norm_sem.at[0])
    for k in range(m):
        @pl.when(place == k)
        def _(k=k):
            for way, count in enumerate(sent(m, pieces, k)):
                if count:
                    took(held.at[pl.ds(0, count * tall)], send_sem.at[way])


def write_kernel(n, held, factor_gate, factor_up, gain, gate, up, out_gate, out_up, out_gain, sem, small_sem):
    rows = held.shape[0] // (2 * n)
    copies = [
        pltpu.make_async_copy(held.at[pl.ds((a * n + i) * rows, rows)], out.at[pl.ds(i * rows, rows)], sem.at[a, i])
        for i in range(n)
        for a, out in enumerate((gate, up))
    ]
    for i, (source, out) in enumerate(((factor_gate, out_gate), (factor_up, out_up), (gain, out_gain))):
        copies.append(pltpu.make_async_copy(source, out, small_sem.at[i]))
    for copy in copies:
        copy.start()
    for copy in copies:
        copy.wait()


def shards(n, parts, one_gate, other_gate, one_up, other_up, mix_share, norm_train, norm_step):
    rows, cols = one_gate.shape
    few = norm_train.shape[0]
    lanes = 128
    padded = -(-rows // lanes) * lanes
    pieces = 2 * max(1, rows // 64)
    gain_shape = (n * parts * few // lanes, lanes)
    kinds = pltpu.SemaphoreType
    vmem, anywhere = pl.BlockSpec(memory_space=pltpu.VMEM), pl.BlockSpec(memory_space=pl.ANY)
    held, factor_gate, factor_up, gain = pl.pallas_call(
        functools.partial(gather_kernel, n, parts, pieces),
        out_shape=(
            pltpu.VMEM((2 * n * rows, cols), jnp.bfloat16),
            pltpu.VMEM((1, cols), jnp.float32),
            pltpu.VMEM((1, cols), jnp.float32),
            pltpu.VMEM(gain_shape, jnp.bfloat16),
        ),
        in_specs=[pl.BlockSpec(memory_space=pltpu.HBM)] * 7,
        out_specs=(vmem,) * 4,
        scratch_shapes=[
            pltpu.VMEM((2, rows, cols), jnp.float32),
            pltpu.VMEM((2, rows, cols), jnp.float32),
            pltpu.VMEM((2, n, 1, cols), jnp.float32),
            pltpu.VMEM((1, padded), jnp.float32),
            pltpu.VMEM((padded, lanes), jnp.float32),
            pltpu.VMEM((2, 1, few), jnp.float32),
            pltpu.VMEM((n * parts, 1, lanes), jnp.float32),
            pltpu.VMEM(gain_shape, jnp.float32),
            kinds.DMA((pieces,)),
            kinds.DMA((2,)),
            kinds.DMA((1,)),
            kinds.DMA((2,)),
            kinds.DMA((3,)),
            kinds.DMA((3,)),
            kinds.DMA((n // 2, pieces)),
            kinds.DMA((1,)),
        ],
        compiler_params=pltpu.CompilerParams(
            collective_id=0, has_side_effects=True, vmem_limit_bytes=46 * 2**20
        ),
        name="mix_gather",
    )(
        one_gate, other_gate, one_up, other_up,
        jnp.pad(mix_share, (0, padded - rows))[None], norm_train[None], norm_step[None],
    )
    gate, up, factor_gate, factor_up, gain = pl.pallas_call(
        functools.partial(write_kernel, n),
        out_shape=(jax.ShapeDtypeStruct((n * rows, cols), jnp.bfloat16),) * 2
        + (jax.ShapeDtypeStruct((1, cols), jnp.float32),) * 2
        + (jax.ShapeDtypeStruct(gain_shape, jnp.bfloat16),),
        in_specs=[vmem] * 4,
        out_specs=(anywhere,) * 5,
        scratch_shapes=[kinds.DMA((2, n)), kinds.DMA((3,))],
        compiler_params=pltpu.CompilerParams(vmem_limit_bytes=2**20),
        name="write_out",
    )(held, factor_gate, factor_up, gain)
    return gate, up, factor_gate[0], factor_up[0], gain.reshape(-1)


def solution(mesh):
    return jax.shard_map(
        functools.partial(shards, mesh.shape["shard"], mesh.shape["tp"]),
        mesh=mesh,
        in_specs=(
            P("shard", "tp"),
            P("shard", "tp"),
            P("shard", "tp"),
            P("shard", "tp"),
            P("shard"),
            P(("shard", "tp")),
            P(("shard", "tp")),
        ),
        out_specs=(P(None, "tp"), P(None, "tp"), P("tp"), P("tp"), P()),
        check_vma=False,
    )
```

time: 180 us -> 177 us (0.983)
  Pallas kernels: 178 us -> 176 us
where the time goes in v1:
time: 177 us
  Pallas kernels  176 us (99%)
    pallas_call x1, Pallas kernels, shards(): pl.pallas_call(functools.partial(gather_kernel, n, parts, pieces), out_sh...  170 us
    pallas_call x1, Pallas kernels, shards(): pl.pallas_call(functools.partial(write_kernel, n), out_shape=(jax.ShapeDt...  6 us

profile of v1, /device:TPU:0, one launch (start us, length us, event | category | flops | bytes accessed | tf_op | source)
XLA Modules:
  0.0 177.0 jit_solution(15266524241044866527)
XLA Ops:
  0.6 170.3 %mix_gather.1 = (bf16[4096,2048]{1,0:T(8,128)(2,1)S(1)}, f32[1,2048]{1,0:T(1,128)S(1)}, f32[1,2048]{1,0:T(1,128)S(1)}, bf16[16,128]{1,0:T(8,128)(2,1)S(1)}) custom-call(f32[256,2048]{1,0:T(8,128)} %one_gate.1, f32[256,2048]{1,0:T(8,128)} %other_gate.1, f32[256,2048]{1,0:T(8,128)} %one_up.1, f32[256,2048]{1,0:T(8,128)} %other_up.1, f32[1,256]{1,0:T(1,128)} %bitcast.6, ...), custom_call_target="tpu_custom_call" | custom-call | tf_op jit(solution)/shard_map/mix_gather/pallas_call | solution.py:305
  171.0 6.0 %write_out.1 = (bf16[2048,2048]{1,0:T(8,128)(2,1)}, bf16[2048,2048]{1,0:T(8,128)(2,1)}, f32[1,2048]{1,0:T(1,128)}, f32[1,2048]{1,0:T(1,128)}, bf16[16,128]{1,0:T(8,128)(2,1)}) custom-call(bf16[4096,2048]{1,0:T(8,128)(2,1)S(1)} %get-tuple-element.14.held, f32[1,2048]{1,0:T(1,128)S(1)} %get-tuple-element.15.factor_gate, ...), custom_call_target="tpu_custom_call" | custom-call | tf_op jit(solution)/shard_map/write_out/pallas_call | solution.py:341

commit v2 on v1

--- a/solution.py
+++ b/solution.py
@@ -10,6 +10,7 @@
 
 MESH = pl.DeviceIdType.MESH
 UP, DOWN, ACROSS = 0, 1, 2
+AHEAD = 3
 
 
 def crosses(place, m, pieces, j, c):
@@ -33,10 +34,10 @@
 
 
 def gather_kernel(
-    n, parts, pieces, one_gate, other_gate, one_up, other_up, mix, train, step,
+    n, parts, pieces, ahead, one_gate, other_gate, one_up, other_up, mix, train, step,
     held, factor_gate, factor_up, gain,
-    ones, others, sums, mix_row, shares, gains, norm, gain_rows,
-    in_sem, small_sem, sum_send, sum_recv, norm_sem, send_sem, recv_sem, rest_sem,
+    ones, others, sums, mix_row, shares, gains, norm, gain_rows, early,
+    early_send, early_recv, in_sem, small_sem, sum_send, sum_recv, norm_sem, send_sem, recv_sem, rest_sem,
 ):
     me = lax.axis_index("shard")
     part = lax.axis_index("tp")
@@ -47,6 +48,8 @@
     mine = me * parts + part
     lanes = shares.shape[1]
 
+    read_mix = pltpu.make_async_copy(mix, mix_row, small_sem.at[0])
+    read_mix.start()
     barrier = pltpu.get_barrier_semaphore()
 
     @pl.loop(1, n)
@@ -57,7 +60,6 @@
     def _(off):
         pl.semaphore_signal(barrier, inc=1, device_id={"tp": lax.rem(part + off, parts)}, device_id_type=MESH)
 
-    read_mix = pltpu.make_async_copy(mix, mix_row, small_sem.at[0])
     read_gains = [
         pltpu.make_async_copy(source, gains.at[i], small_sem.at[1]) for i, source in enumerate((train, step))
     ]
@@ -73,7 +75,6 @@
     def took(ref, sem):
         pltpu.make_async_copy(ref, ref, sem).wait()
 
-    read_mix.start()
     for piece in range(half):
         for copy in reads(piece):
             copy.start()
@@ -84,6 +85,12 @@
         total = jnp.zeros((8, cols), jnp.float32)
         for piece in range(a * half, (a + 1) * half):
             took(ones.at[:, pl.ds(0, tall)], in_sem.at[piece])
+            if piece == half - 1:
+                for later in range(half, pieces):
+                    for copy in reads(later):
+                        copy.start()
+                for copy in read_gains:
+                    copy.start()
 
             def mixed(r, total):
                 at = pl.ds(pl.multiple_of(piece % half * tall + r * 8, 8), 8)
@@ -129,25 +136,45 @@
             device_id={"shard": lax.rem(me + off, n)}, device_id_type=MESH,
         )
 
-    def piece_of(j, s, c):
-        at = pl.multiple_of((c // half * n + 2 * j + s) * rows + c % half * tall, 8)
-        return held.at[pl.ds(at, tall)]
-
-    def send(way, j, s, c, rest=False):
-        target = {
-            UP: {"shard": lax.rem(me + 2, n)},
-            DOWN: {"shard": lax.rem(me + n - 2, n)},
-            ACROSS: {"shard": 2 * place + 1 - side},
-        }[way]
-        block = piece_of(j, s, c)
+    def piece_of(j, s, c, skip=0):
+        at = pl.multiple_of((c // half * n + 2 * j + s) * rows + c % half * tall + skip, 8)
+        return held.at[pl.ds(at, tall - skip)]
+
+    targets = {
+        UP: {"shard": lax.rem(me + 2, n)},
+        DOWN: {"shard": lax.rem(me + n - 2, n)},
+        ACROSS: {"shard": 2 * place + 1 - side},
+    }
+
+    def send(way, j, s, c, rest=False, skip=0):
+        block = piece_of(j, s, c, skip)
         return pltpu.make_async_remote_copy(
             src_ref=block, dst_ref=block,
             send_sem=send_sem.at[way], recv_sem=rest_sem.at[0] if rest else recv_sem.at[j, c],
-            device_id=target, device_id_type=MESH,
-        )
-
-    def arrived(j, s, c):
-        took(piece_of(j, s, c), recv_sem.at[j, c])
+            device_id=targets[way], device_id_type=MESH,
+        )
+
+    def arrived(j, s, c, first):
+        @pl.when(first)
+        def _():
+            took(piece_of(j, s, c, ahead), recv_sem.at[j, c])
+
+        @pl.when(~first)
+        def _():
+            took(piece_of(j, s, c), recv_sem.at[j, c])
+
+    def send_early(way):
+        return pltpu.make_async_remote_copy(
+            src_ref=ones.at[0, pl.ds(0, ahead)], dst_ref=early.at[way],
+            send_sem=early_send.at[0], recv_sem=early_recv.at[way],
+            device_id=targets[way], device_id_type=MESH,
+        )
+
+    def take_early(way, j, s, scale):
+        took(early.at[way], early_recv.at[way])
+        for r in range(0, ahead, 8):
+            there = pl.multiple_of((2 * j + s) * rows + r, 8)
+            held[pl.ds(there, 8)] = (early[way, pl.ds(r, 8)] * scale).astype(jnp.bfloat16)
 
     last = m - 1
     first_place, last_place = place == 0, place == last
@@ -156,6 +183,7 @@
         scale = scales(a)
         for c in range(a * half, (a + 1) * half):
             at = c % half * tall
+            skip = ahead if c == 0 else 0
 
             def scaled(r, _):
                 here = pl.multiple_of(at + r * 8, 8)
@@ -163,27 +191,38 @@
                 held[pl.ds(there, 8)] = (ones[a, pl.ds(here, 8)] * scale).astype(jnp.bfloat16)
                 return 0
 
-            lax.fori_loop(0, tall // 8, scaled, 0, unroll=4)
+            lax.fori_loop(skip // 8, tall // 8, scaled, 0, unroll=tall // 8 % 4 == 0 and skip == 0 and 4 or 1)
 
             @pl.when(~last_place)
             def _():
-                send(UP, place, side, c).start()
+                send(UP, place, side, c, False, skip).start()
 
             @pl.when(~first_place)
             def _():
-                send(DOWN, place, side, c).start()
-
-            send(ACROSS, place, side, c).start()
+                send(DOWN, place, side, c, False, skip).start()
+
+            send(ACROSS, place, side, c, False, skip).start()
+        return scale
 
     mix_and_sum(0)
     pl.semaphore_wait(barrier, n + parts - 2)
     exchange(0)
-    for piece in range(half, pieces):
-        for copy in reads(piece):
-            copy.start()
-    for copy in read_gains:
-        copy.start()
-    own(0)
+
+    @pl.when(~last_place)
+    def _():
+        send_early(UP).start()
+
+    @pl.when(~first_place)
+    def _():
+        send_early(DOWN).start()
+
+    send_early(ACROSS).start()
+    mix_and_sum(1)
+    exchange(1)
+    scale = own(0)
+    for r in range(0, ahead, 8):
+        there = pl.multiple_of(me * rows + r, 8)
+        held[pl.ds(there, 8)] = (ones[0, pl.ds(r, 8)] * scale).astype(jnp.bfloat16)
     took(gains, small_sem.at[1])
     few = gains.shape[2]
     per = lanes // few
@@ -195,16 +234,70 @@
     def _(off):
         norm_row(off).start()
 
-    mix_and_sum(1)
-    exchange(1)
-
+    @pl.when(~first_place)
+    def _():
+        take_early(UP, place - 1, side, scale)
+
+    @pl.when(~last_place)
+    def _():
+        take_early(DOWN, place + 1, side, scale)
+
+    take_early(ACROSS, place, 1 - side, scale)
+    own(1)
     took(norm.at[pl.ds(0, parts - 1)], norm_sem.at[1])
 
     @pl.loop(1, n)
     def _(off):
         norm_group(off).start()
 
-    own(1)
+    def ends(b, c):
+        return (first_place | last_place) & (b == 1)
+
+    def inner(b, c):
+        return ((place == 1) | (place == last - 1)) & (b == last - 1) & (c >= half)
+
+    @pl.loop(0, last * pieces)
+    def _(slot):
+        b, c = slot // pieces, slot % pieces
+
+        @pl.when(b < place)
+        def _():
+            j = place - 1 - b
+            arrived(j, side, c, (b == 0) & (c == 0))
+
+            @pl.when(~last_place)
+            def _():
+                send(UP, j, side, c).start()
+
+            @pl.when(crosses(place, m, pieces, j, c))
+            def _():
+                send(ACROSS, j, side, c, True).start()
+
+        @pl.when(b < last - place)
+        def _():
+            j = place + 1 + b
+            arrived(j, side, c, (b == 0) & (c == 0))
+
+            @pl.when(~first_place)
+            def _():
+                send(DOWN, j, side, c).start()
+
+            @pl.when(crosses(place, m, pieces, j, c))
+            def _():
+                send(ACROSS, j, side, c, True).start()
+
+        @pl.when(ends(b, c) | inner(b, c))
+        def _():
+            arrived(place, 1 - side, c, c == 0)
+
+            @pl.when(first_place | (place == last - 1))
+            def _():
+                send(UP, place, 1 - side, c, True).start()
+
+            @pl.when(last_place | (place == 1))
+            def _():
+                send(DOWN, place, 1 - side, c, True).start()
+
     took(norm.at[pl.ds(0, (n - 1) * parts)], norm_sem.at[2])
 
     @pl.loop(0, gain.shape[0])
@@ -213,69 +306,30 @@
 
     gain[...] = gain_rows[...].astype(jnp.bfloat16)
 
-    def ends(b, c):
-        return (first_place | last_place) & (b == 1)
-
-    def inner(b, c):
-        return ((place == 1) | (place == last - 1)) & (b == last - 1) & (c >= half)
-
-    @pl.loop(0, last * pieces)
-    def _(slot):
-        b, c = slot // pieces, slot % pieces
-
-        @pl.when(b < place)
-        def _():
-            j = place - 1 - b
-            arrived(j, side, c)
-
-            @pl.when(~last_place)
-            def _():
-                send(UP, j, side, c).start()
-
-            @pl.when(crosses(place, m, pieces, j, c))
-            def _():
-                send(ACROSS, j, side, c, True).start()
-
-        @pl.when(b < last - place)
-        def _():
-            j = place + 1 + b
-            arrived(j, side, c)
-
-            @pl.when(~first_place)
-            def _():
-                send(DOWN, j, side, c).start()
-
-            @pl.when(crosses(place, m, pieces, j, c))
-            def _():
-                send(ACROSS, j, side, c, True).start()
-
-        @pl.when(ends(b, c) | inner(b, c))
-        def _():
-            arrived(place, 1 - side, c)
-
-            @pl.when(first_place | (place == last - 1))
-            def _():
-                send(UP, place, 1 - side, c, True).start()
-
-            @pl.when(last_place | (place == 1))
-            def _():
-                send(DOWN, place, 1 - side, c, True).start()
-
     @pl.loop(0, pieces)
     def _(c):
         @pl.when(~(first_place | last_place | (((place == 1) | (place == last - 1)) & (c >= half))))
         def _():
-            arrived(place, 1 - side, c)
+            arrived(place, 1 - side, c, c == 0)
 
     took(held.at[pl.ds(0, last * pieces * tall)], rest_sem.at[0])
     took(sums.at[:, pl.ds(0, n - 1)], sum_send.at[0])
     took(norm.at[pl.ds(0, n * parts - 1)], norm_sem.at[0])
+
+    @pl.when(first_place | last_place)
+    def _():
+        took(early.at[pl.ds(0, 2)], early_send.at[0])
+
+    @pl.when(~(first_place | last_place))
+    def _():
+        took(early, early_send.at[0])
+
     for k in range(m):
         @pl.when(place == k)
         def _(k=k):
             for way, count in enumerate(sent(m, pieces, k)):
                 if count:
-                    took(held.at[pl.ds(0, count * tall)], send_sem.at[way])
+                    took(held.at[pl.ds(0, count * tall - ahead)], send_sem.at[way])
 
 
 def write_kernel(n, held, factor_gate, factor_up, gain, gate, up, out_gate, out_up, out_gain, sem, small_sem):
@@ -299,11 +353,12 @@
     lanes = 128
     padded = -(-rows // lanes) * lanes
     pieces = 2 * max(1, rows // 64)
+    ahead = rows // (pieces // 2) // 8 * AHEAD // 8 * 8
     gain_shape = (n * parts * few // lanes, lanes)
     kinds = pltpu.SemaphoreType
     vmem, anywhere = pl.BlockSpec(memory_space=pltpu.VMEM), pl.BlockSpec(memory_space=pl.ANY)
     held, factor_gate, factor_up, gain = pl.pallas_call(
-        functools.partial(gather_kernel, n, parts, pieces),
+        functools.partial(gather_kernel, n, parts, pieces, ahead),
         out_shape=(
             pltpu.VMEM((2 * n * rows, cols), jnp.bfloat16),
             pltpu.VMEM((1, cols), jnp.float32),
@@ -321,6 +376,9 @@
             pltpu.VMEM((2, 1, few), jnp.float32),
             pltpu.VMEM((n * parts, 1, lanes), jnp.float32),
             pltpu.VMEM(gain_shape, jnp.float32),
+            pltpu.VMEM((3, ahead, cols), jnp.float32),
+            kinds.DMA((1,)),
+            kinds.DMA((3,)),
             kinds.DMA((pieces,)),
             kinds.DMA((2,)),
             kinds.DMA((1,)),

time: 177 us -> 176 us (level)
  no operation moved by 1% of the time
where the time goes in v2:
time: 176 us
  Pallas kernels  175 us (99%)
    pallas_call x1, Pallas kernels, shards(): pl.pallas_call(functools.partial(gather_kernel, n, parts, pieces, ahead),...  169 us
    pallas_call x1, Pallas kernels, shards(): pl.pallas_call(functools.partial(write_kernel, n), out_shape=(jax.ShapeDt...  6 us

profile of v2, /device:TPU:0, one launch (start us, length us, event | category | flops | bytes accessed | tf_op | source)
XLA Modules:
  0.0 176.0 jit_solution(18352063624478793881)
XLA Ops:
  0.6 169.3 %mix_gather.1 = (bf16[4096,2048]{1,0:T(8,128)(2,1)S(1)}, f32[1,2048]{1,0:T(1,128)S(1)}, f32[1,2048]{1,0:T(1,128)S(1)}, bf16[16,128]{1,0:T(8,128)(2,1)S(1)}) custom-call(f32[256,2048]{1,0:T(8,128)} %one_gate.1, f32[256,2048]{1,0:T(8,128)} %other_gate.1, f32[256,2048]{1,0:T(8,128)} %one_up.1, f32[256,2048]{1,0:T(8,128)} %other_up.1, f32[1,256]{1,0:T(1,128)} %bitcast.6, ...), custom_call_target="tpu_custom_call" | custom-call | tf_op jit(solution)/shard_map/mix_gather/pallas_call | solution.py:360
  170.0 6.0 %write_out.1 = (bf16[2048,2048]{1,0:T(8,128)(2,1)}, bf16[2048,2048]{1,0:T(8,128)(2,1)}, f32[1,2048]{1,0:T(1,128)}, f32[1,2048]{1,0:T(1,128)}, bf16[16,128]{1,0:T(8,128)(2,1)}) custom-call(bf16[4096,2048]{1,0:T(8,128)(2,1)S(1)} %get-tuple-element.14.held, f32[1,2048]{1,0:T(1,128)S(1)} %get-tuple-element.15.factor_gate, ...), custom_call_target="tpu_custom_call" | custom-call | tf_op jit(solution)/shard_map/write_out/pallas_call | solution.py:399

commit v3 on v2

--- a/solution.py
+++ b/solution.py
@@ -10,7 +10,7 @@
 
 MESH = pl.DeviceIdType.MESH
 UP, DOWN, ACROSS = 0, 1, 2
-AHEAD = 3
+AHEAD = 2
 
 
 def crosses(place, m, pieces, j, c):
@@ -102,23 +102,27 @@
                 return total + fresh * fresh
 
             total = lax.fori_loop(0, tall // 8, mixed, total, unroll=4)
-        sums[a, me] = jnp.sum(total, axis=0, keepdims=True)
-
-    def sum_copy(a, off):
+        sums[(me, n + m)[a]] = jnp.sum(total, axis=0, keepdims=True)
+
+    def sum_copy(source, target, recv, **device_id):
         return pltpu.make_async_remote_copy(
-            src_ref=sums.at[a, me], dst_ref=sums.at[a, me],
-            send_sem=sum_send.at[0], recv_sem=sum_recv.at[a],
-            device_id={"shard": lax.rem(me + off, n)}, device_id_type=MESH,
-        )
-
-    def exchange(a):
-        @pl.loop(1, n)
+            src_ref=sums.at[source], dst_ref=sums.at[target],
+            send_sem=sum_send.at[0], recv_sem=sum_recv.at[recv],
+            device_id=device_id, device_id_type=MESH,
+        )
+
+    def exchange_up():
+        took(sums.at[0], sum_recv.at[2])
+        sums[n + place] = sums[n + m] + sums[n + m + 1]
+
+        @pl.loop(1, m)
         def _(off):
-            sum_copy(a, off).start()
+            sum_copy(n + place, n + place, 1, shard=lax.rem(me + 2 * off, n)).start()
 
     def scales(a):
-        took(sums.at[a, pl.ds(0, n - 1)], sum_recv.at[a])
-        factors = jnp.sqrt(lax.fori_loop(1, n, lambda i, t: t + sums[a, i], sums[a, 0]))
+        first, count = ((0, n), (n, m))[a]
+        took(sums.at[pl.ds(0, count - 1)], sum_recv.at[a])
+        factors = jnp.sqrt(lax.fori_loop(1, count, lambda i, t: t + sums[first + i], sums[first]))
         (factor_gate, factor_up)[a][...] = factors
         return jnp.broadcast_to(1.0 / factors, (8, cols))
 
@@ -202,11 +206,16 @@
                 send(DOWN, place, side, c, False, skip).start()
 
             send(ACROSS, place, side, c, False, skip).start()
+            if c == (half - 1) // 2:
+                exchange_up()
         return scale
 
     mix_and_sum(0)
     pl.semaphore_wait(barrier, n + parts - 2)
-    exchange(0)
+
+    @pl.loop(1, n)
+    def _(off):
+        sum_copy(me, me, 0, shard=lax.rem(me + off, n)).start()
 
     @pl.when(~last_place)
     def _():
@@ -218,7 +227,7 @@
 
     send_early(ACROSS).start()
     mix_and_sum(1)
-    exchange(1)
+    sum_copy(n + m, n + m + 1, 2, **targets[ACROSS]).start()
     scale = own(0)
     for r in range(0, ahead, 8):
         there = pl.multiple_of(me * rows + r, 8)
@@ -313,7 +322,7 @@
             arrived(place, 1 - side, c, c == 0)
 
     took(held.at[pl.ds(0, last * pieces * tall)], rest_sem.at[0])
-    took(sums.at[:, pl.ds(0, n - 1)], sum_send.at[0])
+    took(sums.at[pl.ds(0, n - 1 + m)], sum_send.at[0])
     took(norm.at[pl.ds(0, n * parts - 1)], norm_sem.at[0])
 
     @pl.when(first_place | last_place)
@@ -332,19 +341,25 @@
                     took(held.at[pl.ds(0, count * tall - ahead)], send_sem.at[way])
 
 
-def write_kernel(n, held, factor_gate, factor_up, gain, gate, up, out_gate, out_up, out_gain, sem, small_sem):
-    rows = held.shape[0] // (2 * n)
+def write_kernel(held, factor_gate, factor_up, gain, gate, up, out_gate, out_up, out_gain, sem, small_sem):
+    half = gate.shape[0]
+    tall = 64
+
+    @pl.loop(0, half // tall)
+    def _(i):
+        at = pl.multiple_of(i * tall, tall)
+        for a, out in enumerate((gate, up)):
+            pltpu.make_async_copy(held.at[pl.ds(a * half + at, tall)], out.at[pl.ds(at, tall)], sem.at[0]).start()
+
     copies = [
-        pltpu.make_async_copy(held.at[pl.ds((a * n + i) * rows, rows)], out.at[pl.ds(i * rows, rows)], sem.at[a, i])
-        for i in range(n)
-        for a, out in enumerate((gate, up))
+        pltpu.make_async_copy(source, out, small_sem.at[i])
+        for i, (source, out) in enumerate(((factor_gate, out_gate), (factor_up, out_up), (gain, out_gain)))
     ]
-    for i, (source, out) in enumerate(((factor_gate, out_gate), (factor_up, out_up), (gain, out_gain))):
-        copies.append(pltpu.make_async_copy(source, out, small_sem.at[i]))
     for copy in copies:
         copy.start()
     for copy in copies:
         copy.wait()
+    pltpu.make_async_copy(held, held, sem.at[0]).wait()
 
 
 def shards(n, parts, one_gate, other_gate, one_up, other_up, mix_share, norm_train, norm_step):
@@ -370,7 +385,7 @@
         scratch_shapes=[
             pltpu.VMEM((2, rows, cols), jnp.float32),
             pltpu.VMEM((2, rows, cols), jnp.float32),
-            pltpu.VMEM((2, n, 1, cols), jnp.float32),
+            pltpu.VMEM((n + n // 2 + 2, 1, cols), jnp.float32),
             pltpu.VMEM((1, padded), jnp.float32),
             pltpu.VMEM((padded, lanes), jnp.float32),
             pltpu.VMEM((2, 1, few), jnp.float32),
@@ -382,7 +397,7 @@
             kinds.DMA((pieces,)),
             kinds.DMA((2,)),
             kinds.DMA((1,)),
-            kinds.DMA((2,)),
+            kinds.DMA((3,)),
             kinds.DMA((3,)),
             kinds.DMA((3,)),
             kinds.DMA((n // 2, pieces)),
@@ -397,13 +412,13 @@
         jnp.pad(mix_share, (0, padded - rows))[None], norm_train[None], norm_step[None],
     )
     gate, up, factor_gate, factor_up, gain = pl.pallas_call(
-        functools.partial(write_kernel, n),
+        write_kernel,
         out_shape=(jax.ShapeDtypeStruct((n * rows, cols), jnp.bfloat16),) * 2
         + (jax.ShapeDtypeStruct((1, cols), jnp.float32),) * 2
         + (jax.ShapeDtypeStruct(gain_shape, jnp.bfloat16),),
         in_specs=[vmem] * 4,
         out_specs=(anywhere,) * 5,
-        scratch_shapes=[kinds.DMA((2, n)), kinds.DMA((3,))],
+        scratch_shapes=[kinds.DMA((1,)), kinds.DMA((3,))],
         compiler_params=pltpu.CompilerParams(vmem_limit_bytes=2**20),
         name="write_out",
     )(held, factor_gate, factor_up, gain)

time: 176 us -> 175 us (level)
  no operation moved by 1% of the time
where the time goes in v3:
time: 175 us
  Pallas kernels  174 us (99%)
    pallas_call x1, Pallas kernels, shards(): pl.pallas_call(functools.partial(gather_kernel, n, parts, pieces, ahead),...  168 us
    pallas_call x1, Pallas kernels, shards(): pl.pallas_call(write_kernel, out_shape=(jax.ShapeDtypeStruct((n * rows, c...  5.8 us

profile of v3, /device:TPU:0, one launch (start us, length us, event | category | flops | bytes accessed | tf_op | source)
XLA Modules:
  0.0 174.6 jit_solution(15641103821099424311)
XLA Ops:
  0.6 168.2 %mix_gather.1 = (bf16[4096,2048]{1,0:T(8,128)(2,1)S(1)}, f32[1,2048]{1,0:T(1,128)S(1)}, f32[1,2048]{1,0:T(1,128)S(1)}, bf16[16,128]{1,0:T(8,128)(2,1)S(1)}) custom-call(f32[256,2048]{1,0:T(8,128)} %one_gate.1, f32[256,2048]{1,0:T(8,128)} %other_gate.1, f32[256,2048]{1,0:T(8,128)} %one_up.1, f32[256,2048]{1,0:T(8,128)} %other_up.1, f32[1,256]{1,0:T(1,128)} %bitcast.6, ...), custom_call_target="tpu_custom_call" | custom-call | tf_op jit(solution)/shard_map/mix_gather/pallas_call | solution.py:375
  168.8 5.8 %write_out.1 = (bf16[2048,2048]{1,0:T(8,128)(2,1)}, bf16[2048,2048]{1,0:T(8,128)(2,1)}, f32[1,2048]{1,0:T(1,128)}, f32[1,2048]{1,0:T(1,128)}, bf16[16,128]{1,0:T(8,128)(2,1)}) custom-call(bf16[4096,2048]{1,0:T(8,128)(2,1)S(1)} %get-tuple-element.14.held, f32[1,2048]{1,0:T(1,128)S(1)} %get-tuple-element.15.factor_gate, ...), custom_call_target="tpu_custom_call" | custom-call | tf_op jit(solution)/shard_map/write_out/pallas_call | solution.py:414

commit v4 on v3

v4 whole, which is shorter than its diff:
```python
import functools

import jax
import jax.numpy as jnp
import numpy as np
from jax import lax
from jax.experimental import pallas as pl
from jax.experimental.pallas import tpu as pltpu
from jax.sharding import PartitionSpec as P

MESH = pl.DeviceIdType.MESH
UP, DOWN, ACROSS = 0, 1, 2
CUTS = (12, 14)


def crosses(place, m, j, c):
    last = m - 1
    kept = ((place == 0) & (j == 1)) | ((place == last) & (j == last - 1))
    kept = kept & (c % 2 == 1)
    return ~(kept | ((place == 1) & (j == 0)) | ((place == last - 1) & (j == last)))


def sent(m, lo, hi, place):
    last, count = m - 1, hi - lo
    extra = count if place in (0, last) else 0
    inner = sum(c % 2 for c in range(lo, hi)) if place in (1, last - 1) else 0
    up = (place + 1) * count * (place != last) + extra * (place == 0) + inner * (place == last - 1)
    down = (m - place) * count * (place != 0) + extra * (place == last) + inner * (place == 1)
    across = count + sum(
        bool(crosses(np.int64(place), m, np.int64(j), np.int64(c)))
        for j in range(m) if j != place for c in range(lo, hi)
    )
    return up, down, across


def cuts_of(pieces):
    return tuple(min(max(1, pieces * cut // 16), pieces - 1) for cut in CUTS)


def took(ref, sem):
    pltpu.make_async_copy(ref, ref, sem).wait()


class Line:
    def __init__(self, n, pieces, rows, ranges, own, land, send_sem, recv_sem, rest_sem, ahead):
        self.n, self.m, self.half = n, n // 2, pieces // 2
        self.rows, self.tall, self.ranges, self.ahead = rows, rows // (pieces // 2), ranges, ahead
        self.me = lax.axis_index("shard")
        self.place, self.side = self.me // 2, self.me % 2
        self.turn = lax.axis_index("tp") % 2
        self.lo, self.hi = (jnp.where(self.turn == 0, first, second) for first, second in zip(*ranges))
        self.base = min(lo for lo, _ in ranges)
        self.own, self.land = own, land
        self.send_sem, self.recv_sem, self.rest_sem = send_sem, recv_sem, rest_sem
        self.first, self.last = self.place == 0, self.place == self.m - 1
        me = self.me
        self.targets = {
            UP: {"shard": lax.rem(me + 2, n)},
            DOWN: {"shard": lax.rem(me + n - 2, n)},
            ACROSS: {"shard": 2 * self.place + 1 - self.side},
        }

    def greet(self, others):
        barrier = pltpu.get_barrier_semaphore()
        for way, unless in ((UP, self.last), (DOWN, self.first), (ACROSS, self.place < 0)):
            @pl.when(~unless)
            def _(way=way):
                pl.semaphore_signal(barrier, inc=1, device_id=self.targets[way], device_id_type=MESH)

        ends = self.first | self.last

        def wait():
            @pl.when(ends)
            def _():
                pl.semaphore_wait(barrier, 2 + others)

            @pl.when(~ends)
            def _():
                pl.semaphore_wait(barrier, 3 + others)

        return wait

    def piece(self, ref, j, s, c, skip=0):
        at = (c // self.half * self.n + 2 * j + s) * self.rows + c % self.half * self.tall + skip
        return ref.at[pl.ds(pl.multiple_of(at, 8), self.tall - skip)]

    def send(self, way, j, s, c, rest=False, skip=0, own=False):
        own = own and self.own is not None
        source = self.own.at[pl.ds(pl.multiple_of((c - self.base) * self.tall, 8), self.tall)] if own else None
        return pltpu.make_async_remote_copy(
            src_ref=self.piece(self.land, j, s, c, skip) if source is None else source,
            dst_ref=self.piece(self.land, j, s, c, skip),
            send_sem=self.send_sem.at[way],
            recv_sem=self.rest_sem.at[0] if rest else self.recv_sem.at[j, c - self.base],
            device_id=self.targets[way], device_id_type=MESH,
        )

    def send_own(self, c, skip=0):
        @pl.when(~self.last)
        def _():
            self.send(UP, self.place, self.side, c, False, skip, True).start()

        @pl.when(~self.first)
        def _():
            self.send(DOWN, self.place, self.side, c, False, skip, True).start()

        self.send(ACROSS, self.place, self.side, c, False, skip, True).start()

    def arrived(self, j, s, c, first):
        def whole():
            took(self.piece(self.land, j, s, c), self.recv_sem.at[j, c - self.base])

        if not self.ahead:
            return whole()

        @pl.when(first)
        def _():
            took(self.piece(self.land, j, s, c, self.ahead), self.recv_sem.at[j, c - self.base])

        pl.when(~first)(whole)

    def relay(self):
        place, side, m, last = self.place, self.side, self.m, self.m - 1
        ends, inner = self.first | self.last, (place == 1) | (place == last - 1)

        @pl.loop(0, last)
        def _(b):
            @pl.loop(self.lo, self.hi)
            def _(c):
                def pass_on(way, j, stop):
                    self.arrived(j, side, c, (b == 0) & (c == 0))

                    @pl.when(~stop)
                    def _():
                        self.send(way, j, side, c).start()

                    @pl.when(crosses(place, m, j, c))
                    def _():
                        self.send(ACROSS, j, side, c, True).start()

                @pl.when(b < place)
                def _():
                    pass_on(UP, place - 1 - b, self.last)

                @pl.when(b < last - place)
                def _():
                    pass_on(DOWN, place + 1 + b, self.first)

                @pl.when((ends & (b == 1)) | (inner & (b == last - 1) & (c % 2 == 1)))
                def _():
                    self.arrived(place, 1 - side, c, c == 0)

                    @pl.when(self.first | (place == last - 1))
                    def _():
                        self.send(UP, place, 1 - side, c, True).start()

                    @pl.when(self.last | (place == 1))
                    def _():
                        self.send(DOWN, place, 1 - side, c, True).start()

    def finish(self):
        place, side, last = self.place, self.side, self.m - 1
        ends, inner = self.first | self.last, (place == 1) | (place == last - 1)

        @pl.loop(self.lo, self.hi)
        def _(c):
            @pl.when(~(ends | (inner & (c % 2 == 1))))
            def _():
                self.arrived(place, 1 - side, c, c == 0)

        for turn, (lo, hi) in enumerate(self.ranges):
            @pl.when(self.turn == turn)
            def _(lo=lo, hi=hi):
                took(self.land.at[pl.ds(0, last * (hi - lo) * self.tall)], self.rest_sem.at[0])
                for k in range(self.m):
                    @pl.when(place == k)
                    def _(k=k):
                        for way, count in enumerate(sent(self.m, lo, hi, k)):
                            if count:
                                took(self.land.at[pl.ds(0, count * self.tall - self.ahead)], self.send_sem.at[way])


def gather_kernel(
    n, parts, pieces, ahead, cuts, one_gate, other_gate, one_up, other_up, mix, train, step,
    held, left, factor_gate, factor_up, gain,
    ones, others, sums, mix_row, shares, gains, norm, gain_rows, early,
    early_send, early_recv, in_sem, small_sem, sum_send, sum_recv, norm_sem, send_sem, recv_sem, rest_sem,
):
    me = lax.axis_index("shard")
    part = lax.axis_index("tp")
    m, half = n // 2, pieces // 2
    place, side = me // 2, me % 2
    rows, cols = ones.shape[1:]
    tall = rows // half
    mine = me * parts + part
    ranges = tuple((0, cut) for cut in cuts)
    line = Line(n, pieces, rows, ranges, None, held, send_sem, recv_sem, rest_sem, ahead)
    targets, first_place, last_place = line.targets, line.first, line.last
    lanes = shares.shape[1]

    read_mix = pltpu.make_async_copy(mix, mix_row, small_sem.at[0])
    read_mix.start()
    barrier = pltpu.get_barrier_semaphore()

    @pl.loop(1, n)
    def _(off):
        pl.semaphore_signal(barrier, inc=1, device_id={"shard": lax.rem(me + off, n)}, device_id_type=MESH)

    @pl.loop(1, parts)
    def _(off):
        pl.semaphore_signal(barrier, inc=1, device_id={"tp": lax.rem(part + off, parts)}, device_id_type=MESH)

    read_gains = [
        pltpu.make_async_copy(source, gains.at[i], small_sem.at[1]) for i, source in enumerate((train, step))
    ]

    def reads(piece):
        a, at = piece // half, pl.ds(piece % half * tall, tall)
        first, second = ((one_gate, other_gate), (one_up, other_up))[a]
        return (
            pltpu.make_async_copy(first.at[at], ones.at[a, at], in_sem.at[piece]),
            pltpu.make_async_copy(second.at[at], others.at[a, at], in_sem.at[piece]),
        )

    for piece in range(half):
        for copy in reads(piece):
            copy.start()
    read_mix.wait()
    shares[...] = jnp.transpose(jnp.broadcast_to(mix_row[...], (lanes, shares.shape[0])))

    def mix_and_sum(a):
        total = jnp.zeros((8, cols), jnp.float32)
        for piece in range(a * half, (a + 1) * half):
            took(ones.at[:, pl.ds(0, tall)], in_sem.at[piece])
            if piece == half - 1:
                for later in range(half, pieces):
                    for copy in reads(later):
                        copy.start()
                for copy in read_gains:
                    copy.start()

            def mixed(r, total):
                at = pl.ds(pl.multiple_of(piece % half * tall + r * 8, 8), 8)
                share = shares[at]
                rest = 1.0 - share
                share, rest = (jnp.concatenate([v] * (cols // lanes), axis=1) for v in (share, rest))
                fresh = share * ones[a, at] + rest * others[a, at]
                ones[a, at] = fresh
                return total + fresh * fresh

            total = lax.fori_loop(0, tall // 8, mixed, total, unroll=4)
        sums[(me, n + m)[a]] = jnp.sum(total, axis=0, keepdims=True)

    def sum_copy(source, target, recv, **device_id):
        return pltpu.make_async_remote_copy(
            src_ref=sums.at[source], dst_ref=sums.at[target],
            send_sem=sum_send.at[0], recv_sem=sum_recv.at[recv],
            device_id=device_id, device_id_type=MESH,
        )

    def exchange_up():
        took(sums.at[0], sum_recv.at[2])
        sums[n + place] = sums[n + m] + sums[n + m + 1]

        @pl.loop(1, m)
        def _(off):
            sum_copy(n + place, n + place, 1, shard=lax.rem(me + 2 * off, n)).start()

    def scales(a):
        first, count = ((0, n), (n, m))[a]
        took(sums.at[pl.ds(0, count - 1)], sum_recv.at[a])
        factors = jnp.sqrt(lax.fori_loop(1, count, lambda i, t: t + sums[first + i], sums[first]))
        (factor_gate, factor_up)[a][...] = factors
        return jnp.broadcast_to(1.0 / factors, (8, cols))

    def norm_row(off):
        return pltpu.make_async_remote_copy(
            src_ref=norm.at[mine], dst_ref=norm.at[mine],
            send_sem=norm_sem.at[0], recv_sem=norm_sem.at[1],
            device_id={"tp": lax.rem(part + off, parts)}, device_id_type=MESH,
        )

    def norm_group(off):
        return pltpu.make_async_remote_copy(
            src_ref=norm.at[pl.ds(me * parts, parts)], dst_ref=norm.at[pl.ds(me * parts, parts)],
            send_sem=norm_sem.at[0], recv_sem=norm_sem.at[2],
            device_id={"shard": lax.rem(me + off, n)}, device_id_type=MESH,
        )

    def send_early(way):
        return pltpu.make_async_remote_copy(
            src_ref=ones.at[0, pl.ds(0, ahead)], dst_ref=early.at[way],
            send_sem=early_send.at[0], recv_sem=early_recv.at[way],
            device_id=targets[way], device_id_type=MESH,
        )

    def take_early(way, j, s, scale):
        took(early.at[way], early_recv.at[way])
        for r in range(0, ahead, 8):
            there = pl.multiple_of((2 * j + s) * rows + r, 8)
            held[pl.ds(there, 8)] = (early[way, pl.ds(r, 8)] * scale).astype(jnp.bfloat16)

    def own(a):
        scale = scales(a)
        for c in range(a * half, (a + 1) * half):
            at = c % half * tall
            skip = ahead if c == 0 else 0

            def scaled(r, _):
                here = pl.multiple_of(at + r * 8, 8)
                there = pl.multiple_of((a * n + me) * rows + at + r * 8, 8)
                fresh = (ones[a, pl.ds(here, 8)] * scale).astype(jnp.bfloat16)
                held[pl.ds(there, 8)] = fresh
                if c >= min(cuts):
                    left[pl.ds(pl.multiple_of((c - min(cuts)) * tall + r * 8, 8), 8)] = fresh
                return 0

            lax.fori_loop(0, tall // 8, scaled, 0, unroll=4)
            if c < max(cuts):
                pl.when(c < line.hi)(functools.partial(line.send_own, c, skip))
            if c == (half - 1) // 2:
                exchange_up()
        return scale

    mix_and_sum(0)
    pl.semaphore_wait(barrier, n + parts - 2)

    @pl.loop(1, n)
    def _(off):
        sum_copy(me, me, 0, shard=lax.rem(me + off, n)).start()

    @pl.when(~last_place)
    def _():
        send_early(UP).start()

    @pl.when(~first_place)
    def _():
        send_early(DOWN).start()

    send_early(ACROSS).start()
    mix_and_sum(1)
    sum_copy(n + m, n + m + 1, 2, **targets[ACROSS]).start()
    scale = own(0)
    took(gains, small_sem.at[1])
    few = gains.shape[2]
    per = lanes // few
    lane = lax.broadcasted_iota(jnp.int32, (1, lanes), 1)
    summed = jnp.concatenate([gains[0] + gains[1]] * per, axis=1)
    norm[mine] = jnp.where(lane // few == mine % per, summed, 0.0)

    @pl.loop(1, parts)
    def _(off):
        norm_row(off).start()

    @pl.when(~first_place)
    def _():
        take_early(UP, place - 1, side, scale)

    @pl.when(~last_place)
    def _():
        take_early(DOWN, place + 1, side, scale)

    take_early(ACROSS, place, 1 - side, scale)
    own(1)
    took(norm.at[pl.ds(0, parts - 1)], norm_sem.at[1])

    @pl.loop(1, n)
    def _(off):
        norm_group(off).start()

    line.relay()
    took(norm.at[pl.ds(0, (n - 1) * parts)], norm_sem.at[2])

    @pl.loop(0, gain.shape[0])
    def _(r):
        gain_rows[pl.ds(r, 1)] = functools.reduce(lambda t, i: t + norm[r * per + i], range(1, per), norm[r * per])

    gain[...] = gain_rows[...].astype(jnp.bfloat16)

    line.finish()
    took(sums.at[pl.ds(0, n - 1 + m)], sum_send.at[0])
    took(norm.at[pl.ds(0, n * parts - 1)], norm_sem.at[0])

    @pl.when(first_place | last_place)
    def _():
        took(early.at[pl.ds(0, 2)], early_send.at[0])

    @pl.when(~(first_place | last_place))
    def _():
        took(early, early_send.at[0])


def rest_kernel(n, pieces, cuts, left, token, more, send_sem, recv_sem, rest_sem):
    rows = more.shape[0] // (2 * n)
    ranges = tuple((cut, pieces) for cut in cuts)
    line = Line(n, pieces, rows, ranges, left, more, send_sem, recv_sem, rest_sem, 0)
    line.greet(0)()
    pl.loop(line.lo, line.hi)(line.send_own)
    line.relay()
    line.finish()


def written(pieces, rows, cut):
    half = pieces // 2
    return [min(max(cut - a * half, 0), half) * (rows // half) for a in range(2)]


def write_kernel(
    n, pieces, cuts, held, factor_gate, factor_up, gain,
    gate, up, out_gate, out_up, out_gain, token, sem, small_sem,
):
    size = gate.shape[0]
    rows = size // n
    me = lax.axis_index("shard")
    token[...] = jnp.zeros_like(token)
    small = [
        pltpu.make_async_copy(source, out, small_sem.at[i])
        for i, (source, out) in enumerate(((factor_gate, out_gate), (factor_up, out_up), (gain, out_gain)))
    ]

    def start(a, at, count):
        at = pl.multiple_of(at, 8)
        pltpu.make_async_copy(held.at[pl.ds(a * size + at, count)], (gate, up)[a].at[pl.ds(at, count)], sem.at[0]).start()

    for turn, cut in enumerate(cuts):
        @pl.when(lax.axis_index("tp") % 2 == turn)
        def _(cut=cut):
            total = 0
            for a, count in enumerate(written(pieces, rows, cut)):
                if count:
                    pl.loop(0, n)(lambda i, a=a, count=count: start(a, i * rows, count))
                if count < rows:
                    start(a, me * rows + count, rows - count)
                total += n * count + rows - count
            for copy in small:
                copy.start()
            for copy in small:
                copy.wait()
            took(held.at[pl.ds(0, total)], sem.at[0])


def write_rest_kernel(n, pieces, cuts, more, gate_in, up_in, gate, up, sem):
    size = gate.shape[0]
    rows = size // n
    me = lax.axis_index("shard")

    def start(a, at, count):
        at = pl.multiple_of(at, 8)
        pltpu.make_async_copy(more.at[pl.ds(a * size + at, count)], (gate, up)[a].at[pl.ds(at, count)], sem.at[0]).start()

    for turn, cut in enumerate(cuts):
        @pl.when(lax.axis_index("tp") % 2 == turn)
        def _(cut=cut):
            total = 0
            for a, count in enumerate(written(pieces, rows, cut)):
                if count < rows:
                    pl.loop(1, n)(
                        lambda i, a=a, count=count: start(a, lax.rem(me + i, n) * rows + count, rows - count)
                    )
                    total += (n - 1) * (rows - count)
            took(more.at[pl.ds(0, total)], sem.at[0])


def shards(n, parts, one_gate, other_gate, one_up, other_up, mix_share, norm_train, norm_step):
    rows, cols = one_gate.shape
    few = norm_train.shape[0]
    lanes = 128
    padded = -(-rows // lanes) * lanes
    pieces = 2 * max(1, rows // 32)
    cuts = cuts_of(pieces)
    ahead = max(8, rows // 16 // 8 * 8)
    gain_shape = (n * parts * few // lanes, lanes)
    kinds = pltpu.SemaphoreType
    vmem, anywhere = pl.BlockSpec(memory_space=pltpu.VMEM), pl.BlockSpec(memory_space=pl.ANY)
    blocks = pltpu.VMEM((2 * n * rows, cols), jnp.bfloat16)
    held, left, factor_gate, factor_up, gain = pl.pallas_call(
        functools.partial(gather_kernel, n, parts, pieces, ahead, cuts),
        out_shape=(
            blocks,
            pltpu.VMEM(((pieces - min(cuts)) * rows // (pieces // 2), cols), jnp.bfloat16),
            pltpu.VMEM((1, cols), jnp.float32),
            pltpu.VMEM((1, cols), jnp.float32),
            pltpu.VMEM(gain_shape, jnp.bfloat16),
        ),
        in_specs=[pl.BlockSpec(memory_space=pltpu.HBM)] * 7,
        out_specs=(vmem,) * 5,
        scratch_shapes=[
            pltpu.VMEM((2, rows, cols), jnp.float32),
            pltpu.VMEM((2, rows, cols), jnp.float32),
            pltpu.VMEM((n + n // 2 + 2, 1, cols), jnp.float32),
            pltpu.VMEM((1, padded), jnp.float32),
            pltpu.VMEM((padded, lanes), jnp.float32),
            pltpu.VMEM((2, 1, few), jnp.float32),
            pltpu.VMEM((n * parts, 1, lanes), jnp.float32),
            pltpu.VMEM(gain_shape, jnp.float32),
            pltpu.VMEM((3, ahead, cols), jnp.float32),
            kinds.DMA((1,)),
            kinds.DMA((3,)),
            kinds.DMA((pieces,)),
            kinds.DMA((2,)),
            kinds.DMA((1,)),
            kinds.DMA((3,)),
            kinds.DMA((3,)),
            kinds.DMA((3,)),
            kinds.DMA((n // 2, max(cuts))),
            kinds.DMA((1,)),
        ],
        compiler_params=pltpu.CompilerParams(
            collective_id=0, has_side_effects=True, vmem_limit_bytes=46 * 2**20
        ),
        name="mix_gather",
    )(
        one_gate, other_gate, one_up, other_up,
        jnp.pad(mix_share, (0, padded - rows))[None], norm_train[None], norm_step[None],
    )
    small = pltpu.CompilerParams(vmem_limit_bytes=2**20)
    whole = (jax.ShapeDtypeStruct((n * rows, cols), jnp.bfloat16),) * 2
    gate, up, factor_gate, factor_up, gain, token = pl.pallas_call(
        functools.partial(write_kernel, n, pieces, cuts),
        out_shape=whole + (jax.ShapeDtypeStruct((1, cols), jnp.float32),) * 2
        + (jax.ShapeDtypeStruct(gain_shape, jnp.bfloat16), pltpu.VMEM((8, lanes), jnp.float32)),
        in_specs=[vmem] * 4,
        out_specs=(anywhere,) * 5 + (vmem,),
        scratch_shapes=[kinds.DMA((1,)), kinds.DMA((3,))],
        compiler_params=small,
        name="write_out",
    )(held, factor_gate, factor_up, gain)
    more = pl.pallas_call(
        functools.partial(rest_kernel, n, pieces, cuts),
        out_shape=blocks,
        in_specs=[vmem] * 2,
        out_specs=vmem,
        scratch_shapes=[kinds.DMA((3,)), kinds.DMA((n // 2, pieces - min(cuts))), kinds.DMA((1,))],
        compiler_params=pltpu.CompilerParams(collective_id=1, has_side_effects=True, vmem_limit_bytes=2**20),
        name="gather_rest",
    )(left, token)
    gate, up = pl.pallas_call(
        functools.partial(write_rest_kernel, n, pieces, cuts),
        out_shape=whole,
        in_specs=[vmem, anywhere, anywhere],
        out_specs=(anywhere,) * 2,
        input_output_aliases={1: 0, 2: 1},
        scratch_shapes=[kinds.DMA((1,))],
        compiler_params=small,
        name="write_rest",
    )(more, gate, up)
    return gate, up, factor_gate[0], factor_up[0], gain.reshape(-1)


def solution(mesh):
    return jax.shard_map(
        functools.partial(shards, mesh.shape["shard"], mesh.shape["tp"]),
        mesh=mesh,
        in_specs=(
            P("shard", "tp"),
            P("shard", "tp"),
            P("shard", "tp"),
            P("shard", "tp"),
            P("shard"),
            P(("shard", "tp")),
            P(("shard", "tp")),
        ),
        out_specs=(P(None, "tp"), P(None, "tp"), P("tp"), P("tp"), P()),
        check_vma=False,
    )
```

time: 175 us -> 172 us (0.983)
  Pallas kernels: 174 us -> 171 us
    pallas_call x2 -> x4, Pallas kernels: 174 us -> 171 us  [the longest x1 131 us: shards(): pl.pallas_call(functools.partial(gather_kernel, n, parts, pieces, ahead,...]
where the time goes in v4:
time: 172 us
  Pallas kernels  171 us (99%)
    pallas_call x1, Pallas kernels, shards(): pl.pallas_call(functools.partial(gather_kernel, n, parts, pieces, ahead,...  131 us
    pallas_call x1, Pallas kernels, shards(): pl.pallas_call(functools.partial(rest_kernel, n, pieces, cuts), out_shape...  33.8 us
    pallas_call x1, Pallas kernels, shards(): pl.pallas_call(functools.partial(write_kernel, n, pieces, cuts), out_shap...  4.75 us

profile of v4, /device:TPU:0, one launch (start us, length us, event | category | flops | bytes accessed | tf_op | source)
XLA Modules:
  0.0 171.8 jit_solution(561006705526059711)
XLA Ops:
  0.6 130.8 %mix_gather.1 = (bf16[4096,2048]{1,0:T(8,128)(2,1)S(1)}, bf16[128,2048]{1,0:T(8,128)(2,1)S(1)}, f32[1,2048]{1,0:T(1,128)S(1)}, f32[1,2048]{1,0:T(1,128)S(1)}, bf16[16,128]{1,0:T(8,128)(2,1)S(1)}) custom-call(f32[256,2048]{1,0:T(8,128)} %one_gate.1, f32[256,2048]{1,0:T(8,128)} %other_gate.1, f32[256,2048]{1,0:T(8,128)} %one_up.1, f32[256,2048]{1,0:T(8,128)} %other_up.1, ...), custom_call_target="tpu_custom_call" | custom-call | tf_op jit(solution)/shard_map/mix_gather/pallas_call | solution.py:476
  131.4 4.8 %write_out.1 = (bf16[2048,2048]{1,0:T(8,128)(2,1)}, bf16[2048,2048]{1,0:T(8,128)(2,1)}, f32[1,2048]{1,0:T(1,128)}, f32[1,2048]{1,0:T(1,128)}, bf16[16,128]{1,0:T(8,128)(2,1)}, /*index=5*/f32[8,128]{1,0:T(8,128)S(1)}) custom-call(bf16[4096,2048]{1,0:T(8,128)(2,1)S(1)} %get-tuple-element.19.held, f32[1,2048]{1,0:T(1,128)S(1)} %get-tuple-element.20.factor_gate, ...), custom_call_target="tpu_custom_call" | custom-call | tf_op jit(solution)/shard_map/write_out/pallas_call | solution.py:518
  136.2 33.8 %gather_rest.1.more = bf16[4096,2048]{1,0:T(8,128)(2,1)S(1)} custom-call(bf16[128,2048]{1,0:T(8,128)(2,1)S(1)} %get-tuple-element.18.left, f32[8,128]{1,0:T(8,128)S(1)} %get-tuple-element.23.token), custom_call_target="tpu_custom_call" | custom-call | tf_op jit(solution)/shard_map/gather_rest/pallas_call | solution.py:528
  170.0 1.9 %write_rest.1 = (bf16[2048,2048]{1,0:T(8,128)(2,1)}, bf16[2048,2048]{1,0:T(8,128)(2,1)}) custom-call(bf16[4096,2048]{1,0:T(8,128)(2,1)S(1)} %gather_rest.1.more, bf16[2048,2048]{1,0:T(8,128)(2,1)} %get-tuple-element.24.gate_in, bf16[2048,2048]{1,0:T(8,128)(2,1)} %get-tuple-element.25.up_in), custom_call_target="tpu_custom_call", output_to_operand_aliasing={{0}: (1, {}), {1}: (2, {})} | custom-call | tf_op jit(solution)/shard_map/write_rest/pallas_call | solution.py:537

commit v5 on v4

--- a/solution.py
+++ b/solution.py
@@ -10,7 +10,7 @@
 
 MESH = pl.DeviceIdType.MESH
 UP, DOWN, ACROSS = 0, 1, 2
-CUTS = (12, 14)
+CUTS = (12, 15)
 
 
 def crosses(place, m, j, c):

time: 172 us -> 170 us (0.988)
  Pallas kernels: 171 us -> 168 us
    pallas_call x1, Pallas kernels: 33.8 us -> 30.7 us  [shards(): pl.pallas_call(functools.partial(rest_kernel, n, pieces, cuts), out_shape...]
where the time goes in v5:
time: 170 us; the launch traced here: 169 us
  Pallas kernels  168 us (99%)
    pallas_call x1, Pallas kernels, shards(): pl.pallas_call(functools.partial(gather_kernel, n, parts, pieces, ahead,...  131 us
    pallas_call x1, Pallas kernels, shards(): pl.pallas_call(functools.partial(rest_kernel, n, pieces, cuts), out_shape...  30.7 us
    pallas_call x1, Pallas kernels, shards(): pl.pallas_call(functools.partial(write_kernel, n, pieces, cuts), out_shap...  4.75 us

profile of v5, /device:TPU:0, one launch (start us, length us, event | category | flops | bytes accessed | tf_op | source)
XLA Modules:
  0.0 168.8 jit_solution(3342220597993922884)
XLA Ops:
  0.6 130.8 %mix_gather.1 = (bf16[4096,2048]{1,0:T(8,128)(2,1)S(1)}, bf16[128,2048]{1,0:T(8,128)(2,1)S(1)}, f32[1,2048]{1,0:T(1,128)S(1)}, f32[1,2048]{1,0:T(1,128)S(1)}, bf16[16,128]{1,0:T(8,128)(2,1)S(1)}) custom-call(f32[256,2048]{1,0:T(8,128)} %one_gate.1, f32[256,2048]{1,0:T(8,128)} %other_gate.1, f32[256,2048]{1,0:T(8,128)} %one_up.1, f32[256,2048]{1,0:T(8,128)} %other_up.1, ...), custom_call_target="tpu_custom_call" | custom-call | tf_op jit(solution)/shard_map/mix_gather/pallas_call | solution.py:476
  131.5 4.8 %write_out.1 = (bf16[2048,2048]{1,0:T(8,128)(2,1)}, bf16[2048,2048]{1,0:T(8,128)(2,1)}, f32[1,2048]{1,0:T(1,128)}, f32[1,2048]{1,0:T(1,128)}, bf16[16,128]{1,0:T(8,128)(2,1)}, /*index=5*/f32[8,128]{1,0:T(8,128)S(1)}) custom-call(bf16[4096,2048]{1,0:T(8,128)(2,1)S(1)} %get-tuple-element.19.held, f32[1,2048]{1,0:T(1,128)S(1)} %get-tuple-element.20.factor_gate, ...), custom_call_target="tpu_custom_call" | custom-call | tf_op jit(solution)/shard_map/write_out/pallas_call | solution.py:518
  136.2 30.7 %gather_rest.1.more = bf16[4096,2048]{1,0:T(8,128)(2,1)S(1)} custom-call(bf16[128,2048]{1,0:T(8,128)(2,1)S(1)} %get-tuple-element.18.left, f32[8,128]{1,0:T(8,128)S(1)} %get-tuple-element.23.token), custom_call_target="tpu_custom_call" | custom-call | tf_op jit(solution)/shard_map/gather_rest/pallas_call | solution.py:528
  166.9 1.9 %write_rest.1 = (bf16[2048,2048]{1,0:T(8,128)(2,1)}, bf16[2048,2048]{1,0:T(8,128)(2,1)}) custom-call(bf16[4096,2048]{1,0:T(8,128)(2,1)S(1)} %gather_rest.1.more, bf16[2048,2048]{1,0:T(8,128)(2,1)} %get-tuple-element.24.gate_in, bf16[2048,2048]{1,0:T(8,128)(2,1)} %get-tuple-element.25.up_in), custom_call_target="tpu_custom_call", output_to_operand_aliasing={{0}: (1, {}), {1}: (2, {})} | custom-call | tf_op jit(solution)/shard_map/write_rest/pallas_call | solution.py:537

commit v6 on v5

--- a/solution.py
+++ b/solution.py
@@ -10,7 +10,7 @@
 
 MESH = pl.DeviceIdType.MESH
 UP, DOWN, ACROSS = 0, 1, 2
-CUTS = (12, 15)
+LATE = ((1, 1), (8, 8))
 
 
 def crosses(place, m, j, c):
@@ -20,21 +20,21 @@
     return ~(kept | ((place == 1) & (j == 0)) | ((place == last - 1) & (j == last)))
 
 
-def sent(m, lo, hi, place):
-    last, count = m - 1, hi - lo
+def sent(m, pieces, late, place):
+    last, count = m - 1, pieces
     extra = count if place in (0, last) else 0
-    inner = sum(c % 2 for c in range(lo, hi)) if place in (1, last - 1) else 0
+    inner = pieces // 2 if place in (1, last - 1) else 0
     up = (place + 1) * count * (place != last) + extra * (place == 0) + inner * (place == last - 1)
     down = (m - place) * count * (place != 0) + extra * (place == last) + inner * (place == 1)
     across = count + sum(
         bool(crosses(np.int64(place), m, np.int64(j), np.int64(c)))
-        for j in range(m) if j != place for c in range(lo, hi)
+        for j in range(m) if j != place for c in range(pieces)
     )
-    return up, down, across
-
-
-def cuts_of(pieces):
-    return tuple(min(max(1, pieces * cut // 16), pieces - 1) for cut in CUTS)
+    return up - late[0] * (place == last - 1), down - late[0] * (place == 1), across - late[1] * (place in (0, last))
+
+
+def late_of(pieces):
+    return tuple((min(along, pieces // 2), min(across, pieces - 1)) for along, across in LATE)
 
 
 def took(ref, sem):
@@ -42,15 +42,14 @@
 
 
 class Line:
-    def __init__(self, n, pieces, rows, ranges, own, land, send_sem, recv_sem, rest_sem, ahead):
+    def __init__(self, n, pieces, rows, lates, land, send_sem, recv_sem, rest_sem, ahead):
         self.n, self.m, self.half = n, n // 2, pieces // 2
-        self.rows, self.tall, self.ranges, self.ahead = rows, rows // (pieces // 2), ranges, ahead
+        self.rows, self.tall, self.pieces, self.lates, self.ahead = rows, rows // (pieces // 2), pieces, lates, ahead
         self.me = lax.axis_index("shard")
         self.place, self.side = self.me // 2, self.me % 2
         self.turn = lax.axis_index("tp") % 2
-        self.lo, self.hi = (jnp.where(self.turn == 0, first, second) for first, second in zip(*ranges))
-        self.base = min(lo for lo, _ in ranges)
-        self.own, self.land = own, land
+        self.along, self.across = (jnp.where(self.turn == 0, *counts) for counts in zip(*lates))
+        self.land = land
         self.send_sem, self.recv_sem, self.rest_sem = send_sem, recv_sem, rest_sem
         self.first, self.last = self.place == 0, self.place == self.m - 1
         me = self.me
@@ -60,62 +59,48 @@
             ACROSS: {"shard": 2 * self.place + 1 - self.side},
         }
 
-    def greet(self, others):
-        barrier = pltpu.get_barrier_semaphore()
-        for way, unless in ((UP, self.last), (DOWN, self.first), (ACROSS, self.place < 0)):
-            @pl.when(~unless)
-            def _(way=way):
-                pl.semaphore_signal(barrier, inc=1, device_id=self.targets[way], device_id_type=MESH)
-
-        ends = self.first | self.last
-
-        def wait():
-            @pl.when(ends)
-            def _():
-                pl.semaphore_wait(barrier, 2 + others)
-
-            @pl.when(~ends)
-            def _():
-                pl.semaphore_wait(barrier, 3 + others)
-
-        return wait
+    def late_along(self, c):
+        return (c % 2 == 1) & (c >= self.pieces - 2 * self.along)
+
+    def late_across(self, j, c):
+        far = jnp.where(self.first, self.m - 1, 0)
+        return (self.first | self.last) & (j == far) & (c >= self.pieces - self.across)
 
     def piece(self, ref, j, s, c, skip=0):
         at = (c // self.half * self.n + 2 * j + s) * self.rows + c % self.half * self.tall + skip
         return ref.at[pl.ds(pl.multiple_of(at, 8), self.tall - skip)]
 
-    def send(self, way, j, s, c, rest=False, skip=0, own=False):
-        own = own and self.own is not None
-        source = self.own.at[pl.ds(pl.multiple_of((c - self.base) * self.tall, 8), self.tall)] if own else None
+    def send(self, way, j, s, c, rest=False, skip=0):
+        block = self.piece(self.land, j, s, c, skip)
         return pltpu.make_async_remote_copy(
-            src_ref=self.piece(self.land, j, s, c, skip) if source is None else source,
-            dst_ref=self.piece(self.land, j, s, c, skip),
-            send_sem=self.send_sem.at[way],
-            recv_sem=self.rest_sem.at[0] if rest else self.recv_sem.at[j, c - self.base],
+            src_ref=block, dst_ref=block,
+            send_sem=self.send_sem.at[way], recv_sem=self.rest_sem.at[0] if rest else self.recv_sem.at[j, c],
             device_id=self.targets[way], device_id_type=MESH,
         )
 
     def send_own(self, c, skip=0):
-        @pl.when(~self.last)
+        late = self.late_along(c)
+
+        @pl.when(~(self.last | ((self.place == self.m - 2) & late)))
         def _():
-            self.send(UP, self.place, self.side, c, False, skip, True).start()
-
-        @pl.when(~self.first)
+            self.send(UP, self.place, self.side, c, False, skip).start()
+
+        @pl.when(~(self.first | ((self.place == 1) & late)))
         def _():
-            self.send(DOWN, self.place, self.side, c, False, skip, True).start()
-
-        self.send(ACROSS, self.place, self.side, c, False, skip, True).start()
+            self.send(DOWN, self.place, self.side, c, False, skip).start()
+
+        self.send(ACROSS, self.place, self.side, c, False, skip).start()
 
     def arrived(self, j, s, c, first):
         def whole():
-            took(self.piece(self.land, j, s, c), self.recv_sem.at[j, c - self.base])
+            took(self.piece(self.land, j, s, c), self.recv_sem.at[j, c])
 
         if not self.ahead:
             return whole()
 
         @pl.when(first)
         def _():
-            took(self.piece(self.land, j, s, c, self.ahead), self.recv_sem.at[j, c - self.base])
+            took(self.piece(self.land, j, s, c, self.ahead), self.recv_sem.at[j, c])
 
         pl.when(~first)(whole)
 
@@ -125,8 +110,10 @@
 
         @pl.loop(0, last)
         def _(b):
-            @pl.loop(self.lo, self.hi)
+            @pl.loop(0, self.pieces)
             def _(c):
+                late = self.late_along(c) & (b == 0)
+
                 def pass_on(way, j, stop):
                     self.arrived(j, side, c, (b == 0) & (c == 0))
 
@@ -134,15 +121,15 @@
                     def _():
                         self.send(way, j, side, c).start()
 
-                    @pl.when(crosses(place, m, j, c))
+                    @pl.when(crosses(place, m, j, c) & ~self.late_across(j, c))
                     def _():
                         self.send(ACROSS, j, side, c, True).start()
 
-                @pl.when(b < place)
+                @pl.when((b < place) & ~(self.last & late))
                 def _():
                     pass_on(UP, place - 1 - b, self.last)
 
-                @pl.when(b < last - place)
+                @pl.when((b < last - place) & ~(self.first & late))
                 def _():
                     pass_on(DOWN, place + 1 + b, self.first)
 
@@ -162,26 +149,25 @@
         place, side, last = self.place, self.side, self.m - 1
         ends, inner = self.first | self.last, (place == 1) | (place == last - 1)
 
-        @pl.loop(self.lo, self.hi)
+        @pl.loop(0, self.pieces)
         def _(c):
             @pl.when(~(ends | (inner & (c % 2 == 1))))
             def _():
                 self.arrived(place, 1 - side, c, c == 0)
 
-        for turn, (lo, hi) in enumerate(self.ranges):
-            @pl.when(self.turn == turn)
-            def _(lo=lo, hi=hi):
-                took(self.land.at[pl.ds(0, last * (hi - lo) * self.tall)], self.rest_sem.at[0])
-                for k in range(self.m):
-                    @pl.when(place == k)
-                    def _(k=k):
-                        for way, count in enumerate(sent(self.m, lo, hi, k)):
-                            if count:
-                                took(self.land.at[pl.ds(0, count * self.tall - self.ahead)], self.send_sem.at[way])
+        for turn, late in enumerate(self.lates):
+            for k in range(self.m):
+                @pl.when((self.turn == turn) & (place == k))
+                def _(late=late, k=k):
+                    rest = last * self.pieces - late[1] * (k in (0, last))
+                    took(self.land.at[pl.ds(0, rest * self.tall)], self.rest_sem.at[0])
+                    for way, count in enumerate(sent(self.m, self.pieces, late, k)):
+                        if count:
+                            took(self.land.at[pl.ds(0, count * self.tall - self.ahead)], self.send_sem.at[way])
 
 
 def gather_kernel(
-    n, parts, pieces, ahead, cuts, one_gate, other_gate, one_up, other_up, mix, train, step,
+    n, parts, pieces, ahead, lates, one_gate, other_gate, one_up, other_up, mix, train, step,
     held, left, factor_gate, factor_up, gain,
     ones, others, sums, mix_row, shares, gains, norm, gain_rows, early,
     early_send, early_recv, in_sem, small_sem, sum_send, sum_recv, norm_sem, send_sem, recv_sem, rest_sem,
@@ -193,8 +179,7 @@
     rows, cols = ones.shape[1:]
     tall = rows // half
     mine = me * parts + part
-    ranges = tuple((0, cut) for cut in cuts)
-    line = Line(n, pieces, rows, ranges, None, held, send_sem, recv_sem, rest_sem, ahead)
+    line = Line(n, pieces, rows, lates, held, send_sem, recv_sem, rest_sem, ahead)
     targets, first_place, last_place = line.targets, line.first, line.last
     lanes = shares.shape[1]
 
@@ -309,15 +294,11 @@
             def scaled(r, _):
                 here = pl.multiple_of(at + r * 8, 8)
                 there = pl.multiple_of((a * n + me) * rows + at + r * 8, 8)
-                fresh = (ones[a, pl.ds(here, 8)] * scale).astype(jnp.bfloat16)
-                held[pl.ds(there, 8)] = fresh
-                if c >= min(cuts):
-                    left[pl.ds(pl.multiple_of((c - min(cuts)) * tall + r * 8, 8), 8)] = fresh
+                held[pl.ds(there, 8)] = (ones[a, pl.ds(here, 8)] * scale).astype(jnp.bfloat16)
                 return 0
 
             lax.fori_loop(0, tall // 8, scaled, 0, unroll=4)
-            if c < max(cuts):
-                pl.when(c < line.hi)(functools.partial(line.send_own, c, skip))
+            line.send_own(c, skip)
             if c == (half - 1) // 2:
                 exchange_up()
         return scale
@@ -368,7 +349,24 @@
     def _(off):
         norm_group(off).start()
 
+    def set_aside(i, j, c):
+        @pl.loop(0, tall // 8)
+        def _(r):
+            at = (c // half * n + 2 * j + side) * rows + c % half * tall + r * 8
+            left[pl.ds(pl.multiple_of(i * tall + r * 8, 8), 8)] = held[pl.ds(pl.multiple_of(at, 8), 8)]
+
+    @pl.when((place == 1) | (place == m - 2))
+    def _():
+        for i in range(max(along for along, _ in lates)):
+            set_aside(i, place, pieces - 1 - 2 * i)
+
     line.relay()
+
+    @pl.when(first_place | last_place)
+    def _():
+        for i in range(max(across for _, across in lates)):
+            set_aside(i, jnp.where(first_place, m - 1, 0), pieces - 1 - i)
+
     took(norm.at[pl.ds(0, (n - 1) * parts)], norm_sem.at[2])
 
     @pl.loop(0, gain.shape[0])
@@ -390,75 +388,92 @@
         took(early, early_send.at[0])
 
 
-def rest_kernel(n, pieces, cuts, left, token, more, send_sem, recv_sem, rest_sem):
-    rows = more.shape[0] // (2 * n)
-    ranges = tuple((cut, pieces) for cut in cuts)
-    line = Line(n, pieces, rows, ranges, left, more, send_sem, recv_sem, rest_sem, 0)
-    line.greet(0)()
-    pl.loop(line.lo, line.hi)(line.send_own)
-    line.relay()
-    line.finish()
-
-
-def written(pieces, rows, cut):
-    half = pieces // 2
-    return [min(max(cut - a * half, 0), half) * (rows // half) for a in range(2)]
+def last_kernel(n, lates, left, token, more, send_sem, recv_sem):
+    tall = left.shape[0] // max(map(max, lates))
+    me, turn = lax.axis_index("shard"), lax.axis_index("tp") % 2
+    place, side, last = me // 2, me % 2, n // 2 - 1
+    ends, nexts = (place == 0) | (place == last), (place == 1) | (place == last - 1)
+    partner = {"shard": 2 * place + 1 - side}
+    inward = {"shard": jnp.where(place == 0, 2, 2 * last - 2) + side}
+    outward = {"shard": jnp.where(place == 1, 0, 2 * last) + side}
+    barrier = pltpu.get_barrier_semaphore()
+
+    @pl.when(ends)
+    def _():
+        for device in (partner, inward):
+            pl.semaphore_signal(barrier, inc=1, device_id=device, device_id_type=MESH)
+        pl.semaphore_wait(barrier, 2)
+
+    @pl.when(nexts)
+    def _():
+        pl.semaphore_signal(barrier, inc=1, device_id=outward, device_id_type=MESH)
+        pl.semaphore_wait(barrier, 1)
+
+    for t, late in enumerate(lates):
+        def copy(which, device, late=late):
+            return pltpu.make_async_remote_copy(
+                src_ref=left.at[pl.ds(0, late[which] * tall)], dst_ref=more.at[which, pl.ds(0, late[which] * tall)],
+                send_sem=send_sem.at[0], recv_sem=recv_sem.at[which],
+                device_id=device, device_id_type=MESH,
+            )
+
+        @pl.when((turn == t) & nexts)
+        def _(copy=copy):
+            along = copy(0, outward)
+            along.start()
+            along.wait_send()
+
+        @pl.when((turn == t) & ends)
+        def _(copy=copy):
+            across = copy(1, partner)
+            across.start()
+            copy(0, inward).wait_recv()
+            across.wait()
 
 
 def write_kernel(
-    n, pieces, cuts, held, factor_gate, factor_up, gain,
-    gate, up, out_gate, out_up, out_gain, token, sem, small_sem,
+    held, factor_gate, factor_up, gain, gate, up, out_gate, out_up, out_gain, token, sem, small_sem,
 ):
     size = gate.shape[0]
-    rows = size // n
-    me = lax.axis_index("shard")
+    tall = 64
     token[...] = jnp.zeros_like(token)
     small = [
         pltpu.make_async_copy(source, out, small_sem.at[i])
         for i, (source, out) in enumerate(((factor_gate, out_gate), (factor_up, out_up), (gain, out_gain)))
     ]
 
-    def start(a, at, count):
-        at = pl.multiple_of(at, 8)
-        pltpu.make_async_copy(held.at[pl.ds(a * size + at, count)], (gate, up)[a].at[pl.ds(at, count)], sem.at[0]).start()
-
-    for turn, cut in enumerate(cuts):
-        @pl.when(lax.axis_index("tp") % 2 == turn)
-        def _(cut=cut):
-            total = 0
-            for a, count in enumerate(written(pieces, rows, cut)):
-                if count:
-                    pl.loop(0, n)(lambda i, a=a, count=count: start(a, i * rows, count))
-                if count < rows:
-                    start(a, me * rows + count, rows - count)
-                total += n * count + rows - count
-            for copy in small:
-                copy.start()
-            for copy in small:
-                copy.wait()
-            took(held.at[pl.ds(0, total)], sem.at[0])
-
-
-def write_rest_kernel(n, pieces, cuts, more, gate_in, up_in, gate, up, sem):
-    size = gate.shape[0]
-    rows = size // n
+    @pl.loop(0, size // tall)
+    def _(i):
+        at = pl.multiple_of(i * tall, tall)
+        for a, out in enumerate((gate, up)):
+            pltpu.make_async_copy(held.at[pl.ds(a * size + at, tall)], out.at[pl.ds(at, tall)], sem.at[0]).start()
+
+    for copy in small:
+        copy.start()
+    for copy in small:
+        copy.wait()
+    took(held, sem.at[0])
+
+
+def write_last_kernel(n, pieces, lates, more, gate_in, up_in, gate, up, sem):
+    half = pieces // 2
+    rows = gate.shape[0] // n
+    tall = rows // half
     me = lax.axis_index("shard")
-
-    def start(a, at, count):
-        at = pl.multiple_of(at, 8)
-        pltpu.make_async_copy(more.at[pl.ds(a * size + at, count)], (gate, up)[a].at[pl.ds(at, count)], sem.at[0]).start()
-
-    for turn, cut in enumerate(cuts):
-        @pl.when(lax.axis_index("tp") % 2 == turn)
-        def _(cut=cut):
-            total = 0
-            for a, count in enumerate(written(pieces, rows, cut)):
-                if count < rows:
-                    pl.loop(1, n)(
-                        lambda i, a=a, count=count: start(a, lax.rem(me + i, n) * rows + count, rows - count)
-                    )
-                    total += (n - 1) * (rows - count)
-            took(more.at[pl.ds(0, total)], sem.at[0])
+    place, side, last = me // 2, me % 2, n // 2 - 1
+    near, far = jnp.where(place == 0, 1, last - 1), jnp.where(place == 0, last, 0)
+
+    for turn, late in enumerate(lates):
+        @pl.when((lax.axis_index("tp") % 2 == turn) & ((place == 0) | (place == last)))
+        def _(late=late):
+            for which, (j, s, step) in enumerate(((near, side, 2), (far, 1 - side, 1))):
+                for i in range(late[which]):
+                    c = pieces - 1 - step * i
+                    at = pl.multiple_of((2 * j + s) * rows + c % half * tall, 8)
+                    pltpu.make_async_copy(
+                        more.at[which, pl.ds(i * tall, tall)], (gate, up)[c // half].at[pl.ds(at, tall)], sem.at[0]
+                    ).start()
+            took(gate.at[pl.ds(0, sum(late) * tall)], sem.at[0])
 
 
 def shards(n, parts, one_gate, other_gate, one_up, other_up, mix_share, norm_train, norm_step):
@@ -467,17 +482,18 @@
     lanes = 128
     padded = -(-rows // lanes) * lanes
     pieces = 2 * max(1, rows // 32)
-    cuts = cuts_of(pieces)
+    lates = late_of(pieces)
+    aside = max(map(max, lates)) * rows // (pieces // 2)
     ahead = max(8, rows // 16 // 8 * 8)
     gain_shape = (n * parts * few // lanes, lanes)
     kinds = pltpu.SemaphoreType
     vmem, anywhere = pl.BlockSpec(memory_space=pltpu.VMEM), pl.BlockSpec(memory_space=pl.ANY)
     blocks = pltpu.VMEM((2 * n * rows, cols), jnp.bfloat16)
     held, left, factor_gate, factor_up, gain = pl.pallas_call(
-        functools.partial(gather_kernel, n, parts, pieces, ahead, cuts),
+        functools.partial(gather_kernel, n, parts, pieces, ahead, lates),
         out_shape=(
             blocks,
-            pltpu.VMEM(((pieces - min(cuts)) * rows // (pieces // 2), cols), jnp.bfloat16),
+            pltpu.VMEM((aside, cols), jnp.bfloat16),
             pltpu.VMEM((1, cols), jnp.float32),
             pltpu.VMEM((1, cols), jnp.float32),
             pltpu.VMEM(gain_shape, jnp.bfloat16),
@@ -502,7 +518,7 @@
             kinds.DMA((3,)),
             kinds.DMA((3,)),
             kinds.DMA((3,)),
-            kinds.DMA((n // 2, max(cuts))),
+            kinds.DMA((n // 2, pieces)),
             kinds.DMA((1,)),
         ],
         compiler_params=pltpu.CompilerParams(
@@ -516,7 +532,7 @@
     small = pltpu.CompilerParams(vmem_limit_bytes=2**20)
     whole = (jax.ShapeDtypeStruct((n * rows, cols), jnp.bfloat16),) * 2
     gate, up, factor_gate, factor_up, gain, token = pl.pallas_call(
-        functools.partial(write_kernel, n, pieces, cuts),
+        write_kernel,
         out_shape=whole + (jax.ShapeDtypeStruct((1, cols), jnp.float32),) * 2
         + (jax.ShapeDtypeStruct(gain_shape, jnp.bfloat16), pltpu.VMEM((8, lanes), jnp.float32)),
         in_specs=[vmem] * 4,
@@ -526,23 +542,23 @@
         name="write_out",
     )(held, factor_gate, factor_up, gain)
     more = pl.pallas_call(
-        functools.partial(rest_kernel, n, pieces, cuts),
-        out_shape=blocks,
+        functools.partial(last_kernel, n, lates),
+        out_shape=pltpu.VMEM((2, aside, cols), jnp.bfloat16),
         in_specs=[vmem] * 2,
         out_specs=vmem,
-        scratch_shapes=[kinds.DMA((3,)), kinds.DMA((n // 2, pieces - min(cuts))), kinds.DMA((1,))],
+        scratch_shapes=[kinds.DMA((1,)), kinds.DMA((2,))],
         compiler_params=pltpu.CompilerParams(collective_id=1, has_side_effects=True, vmem_limit_bytes=2**20),
-        name="gather_rest",
+        name="gather_last",
     )(left, token)
     gate, up = pl.pallas_call(
-        functools.partial(write_rest_kernel, n, pieces, cuts),
+        functools.partial(write_last_kernel, n, pieces, lates),
         out_shape=whole,
         in_specs=[vmem, anywhere, anywhere],
         out_specs=(anywhere,) * 2,
         input_output_aliases={1: 0, 2: 1},
         scratch_shapes=[kinds.DMA((1,))],
         compiler_params=small,
-        name="write_rest",
+        name="write_last",
     )(more, gate, up)
     return gate, up, factor_gate[0], factor_up[0], gain.reshape(-1)
 

time: 170 us -> 170 us (level)
    pallas_call x1, Pallas kernels: 131 us -> 156 us  [shards(): pl.pallas_call(functools.partial(gather_kernel, n, parts, pieces, ahead,...]
    pallas_call x3, Pallas kernels: 37.3 us -> 13 us  [the longest x1 6.45 us: shards(): pl.pallas_call(functools.partial(last_kernel, n, lates), out_shape=pltpu....]
where the time goes in v6:
time: 170 us; the launch traced here: 169 us
  Pallas kernels  169 us (99%)
    pallas_call x1, Pallas kernels, shards(): pl.pallas_call(functools.partial(gather_kernel, n, parts, pieces, ahead,...  156 us
    pallas_call x1, Pallas kernels, shards(): pl.pallas_call(functools.partial(last_kernel, n, lates), out_shape=pltpu....  6.45 us
    pallas_call x1, Pallas kernels, shards(): pl.pallas_call(write_kernel, out_shape=whole + (jax.ShapeDtypeStruct((1,...  5.8 us

profile of v6, /device:TPU:0, one launch (start us, length us, event | category | flops | bytes accessed | tf_op | source)
XLA Modules:
  0.0 169.5 jit_solution(17929314592832091834)
XLA Ops:
  0.6 155.8 %mix_gather.1 = (bf16[4096,2048]{1,0:T(8,128)(2,1)S(1)}, bf16[256,2048]{1,0:T(8,128)(2,1)S(1)}, f32[1,2048]{1,0:T(1,128)S(1)}, f32[1,2048]{1,0:T(1,128)S(1)}, bf16[16,128]{1,0:T(8,128)(2,1)S(1)}) custom-call(f32[256,2048]{1,0:T(8,128)} %one_gate.1, f32[256,2048]{1,0:T(8,128)} %other_gate.1, f32[256,2048]{1,0:T(8,128)} %one_up.1, f32[256,2048]{1,0:T(8,128)} %other_up.1, ...), custom_call_target="tpu_custom_call" | custom-call | tf_op jit(solution)/shard_map/mix_gather/pallas_call | solution.py:492
  156.5 5.8 %write_out.1 = (bf16[2048,2048]{1,0:T(8,128)(2,1)}, bf16[2048,2048]{1,0:T(8,128)(2,1)}, f32[1,2048]{1,0:T(1,128)}, f32[1,2048]{1,0:T(1,128)}, bf16[16,128]{1,0:T(8,128)(2,1)}, /*index=5*/f32[8,128]{1,0:T(8,128)S(1)}) custom-call(bf16[4096,2048]{1,0:T(8,128)(2,1)S(1)} %get-tuple-element.19.held, f32[1,2048]{1,0:T(1,128)S(1)} %get-tuple-element.20.factor_gate, ...), custom_call_target="tpu_custom_call" | custom-call | tf_op jit(solution)/shard_map/write_out/pallas_call | solution.py:534
  162.3 6.4 %gather_last.1.more = bf16[2,256,2048]{2,1,0:T(8,128)(2,1)S(1)} custom-call(bf16[256,2048]{1,0:T(8,128)(2,1)S(1)} %get-tuple-element.18.left, f32[8,128]{1,0:T(8,128)S(1)} %get-tuple-element.23.token), custom_call_target="tpu_custom_call" | custom-call | tf_op jit(solution)/shard_map/gather_last/pallas_call | solution.py:544
  168.7 0.7 write_last.1

commit v7 on v6

--- a/solution.py
+++ b/solution.py
@@ -10,7 +10,7 @@
 
 MESH = pl.DeviceIdType.MESH
 UP, DOWN, ACROSS = 0, 1, 2
-LATE = ((1, 1), (8, 8))
+LATE = ((1, 1), (10, 10))
 
 
 def crosses(place, m, j, c):
@@ -34,7 +34,7 @@
 
 
 def late_of(pieces):
-    return tuple((min(along, pieces // 2), min(across, pieces - 1)) for along, across in LATE)
+    return tuple((min(along, pieces // 2 + pieces // 4), min(across, pieces - 1)) for along, across in LATE)
 
 
 def took(ref, sem):
@@ -62,6 +62,9 @@
     def late_along(self, c):
         return (c % 2 == 1) & (c >= self.pieces - 2 * self.along)
 
+    def late_passed(self, c):
+        return (c % 2 == 1) & (c >= 2 * self.pieces - 2 * self.along)
+
     def late_across(self, j, c):
         far = jnp.where(self.first, self.m - 1, 0)
         return (self.first | self.last) & (j == far) & (c >= self.pieces - self.across)
@@ -136,12 +139,13 @@
                 @pl.when((ends & (b == 1)) | (inner & (b == last - 1) & (c % 2 == 1)))
                 def _():
                     self.arrived(place, 1 - side, c, c == 0)
-
-                    @pl.when(self.first | (place == last - 1))
+                    now = ~(inner & self.late_passed(c))
+
+                    @pl.when((self.first | (place == last - 1)) & now)
                     def _():
                         self.send(UP, place, 1 - side, c, True).start()
 
-                    @pl.when(self.last | (place == 1))
+                    @pl.when((self.last | (place == 1)) & now)
                     def _():
                         self.send(DOWN, place, 1 - side, c, True).start()
 
@@ -159,7 +163,8 @@
             for k in range(self.m):
                 @pl.when((self.turn == turn) & (place == k))
                 def _(late=late, k=k):
-                    rest = last * self.pieces - late[1] * (k in (0, last))
+                    passed = max(0, late[0] - self.pieces // 2)
+                    rest = last * self.pieces - (late[1] + passed) * (k in (0, last))
                     took(self.land.at[pl.ds(0, rest * self.tall)], self.rest_sem.at[0])
                     for way, count in enumerate(sent(self.m, self.pieces, late, k)):
                         if count:
@@ -349,18 +354,18 @@
     def _(off):
         norm_group(off).start()
 
-    def set_aside(i, j, c):
+    def set_aside(i, j, c, side=side):
         @pl.loop(0, tall // 8)
         def _(r):
             at = (c // half * n + 2 * j + side) * rows + c % half * tall + r * 8
             left[pl.ds(pl.multiple_of(i * tall + r * 8, 8), 8)] = held[pl.ds(pl.multiple_of(at, 8), 8)]
 
+    line.relay()
+
     @pl.when((place == 1) | (place == m - 2))
     def _():
         for i in range(max(along for along, _ in lates)):
-            set_aside(i, place, pieces - 1 - 2 * i)
-
-    line.relay()
+            set_aside(i, place, pieces - 1 - 2 * (i % half), (side, 1 - side)[i // half])
 
     @pl.when(first_place | last_place)
     def _():
@@ -468,8 +473,9 @@
         def _(late=late):
             for which, (j, s, step) in enumerate(((near, side, 2), (far, 1 - side, 1))):
                 for i in range(late[which]):
-                    c = pieces - 1 - step * i
-                    at = pl.multiple_of((2 * j + s) * rows + c % half * tall, 8)
+                    c = pieces - 1 - step * (i % half if step == 2 else i)
+                    here = 1 - s if step == 2 and i >= half else s
+                    at = pl.multiple_of((2 * j + here) * rows + c % half * tall, 8)
                     pltpu.make_async_copy(
                         more.at[which, pl.ds(i * tall, tall)], (gate, up)[c // half].at[pl.ds(at, tall)], sem.at[0]
                     ).start()

time: 170 us -> 169 us (level)
  Pallas kernels: 169 us -> 167 us
where the time goes in v7:
time: 169 us; the launch traced here: 168 us
  Pallas kernels  167 us (99%)
    pallas_call x1, Pallas kernels, shards(): pl.pallas_call(functools.partial(gather_kernel, n, parts, pieces, ahead,...  154 us
    pallas_call x1, Pallas kernels, shards(): pl.pallas_call(functools.partial(last_kernel, n, lates), out_shape=pltpu....  6.45 us
    pallas_call x1, Pallas kernels, shards(): pl.pallas_call(write_kernel, out_shape=whole + (jax.ShapeDtypeStruct((1,...  5.8 us

profile of v7, /device:TPU:0, one launch (start us, length us, event | category | flops | bytes accessed | tf_op | source)
XLA Modules:
  0.0 167.9 jit_solution(17709055863215369584)
XLA Ops:
  0.6 154.2 %mix_gather.1 = (bf16[4096,2048]{1,0:T(8,128)(2,1)S(1)}, bf16[320,2048]{1,0:T(8,128)(2,1)S(1)}, f32[1,2048]{1,0:T(1,128)S(1)}, f32[1,2048]{1,0:T(1,128)S(1)}, bf16[16,128]{1,0:T(8,128)(2,1)S(1)}) custom-call(f32[256,2048]{1,0:T(8,128)} %one_gate.1, f32[256,2048]{1,0:T(8,128)} %other_gate.1, f32[256,2048]{1,0:T(8,128)} %one_up.1, f32[256,2048]{1,0:T(8,128)} %other_up.1, ...), custom_call_target="tpu_custom_call" | custom-call | tf_op jit(solution)/shard_map/mix_gather/pallas_call | solution.py:498
  154.9 5.8 %write_out.1 = (bf16[2048,2048]{1,0:T(8,128)(2,1)}, bf16[2048,2048]{1,0:T(8,128)(2,1)}, f32[1,2048]{1,0:T(1,128)}, f32[1,2048]{1,0:T(1,128)}, bf16[16,128]{1,0:T(8,128)(2,1)}, /*index=5*/f32[8,128]{1,0:T(8,128)S(1)}) custom-call(bf16[4096,2048]{1,0:T(8,128)(2,1)S(1)} %get-tuple-element.19.held, f32[1,2048]{1,0:T(1,128)S(1)} %get-tuple-element.20.factor_gate, ...), custom_call_target="tpu_custom_call" | custom-call | tf_op jit(solution)/shard_map/write_out/pallas_call | solution.py:540
  160.7 6.4 %gather_last.1.more = bf16[2,320,2048]{2,1,0:T(8,128)(2,1)S(1)} custom-call(bf16[320,2048]{1,0:T(8,128)(2,1)S(1)} %get-tuple-element.18.left, f32[8,128]{1,0:T(8,128)S(1)} %get-tuple-element.23.token), custom_call_target="tpu_custom_call" | custom-call | tf_op jit(solution)/shard_map/gather_last/pallas_call | solution.py:550
  167.1 0.7 write_last.1

commit v8 on v7

--- a/solution.py
+++ b/solution.py
@@ -184,6 +184,7 @@
     rows, cols = ones.shape[1:]
     tall = rows // half
     mine = me * parts + part
+    group = 2 - half % 2
     line = Line(n, pieces, rows, lates, held, send_sem, recv_sem, rest_sem, ahead)
     targets, first_place, last_place = line.targets, line.first, line.last
     lanes = shares.shape[1]
@@ -208,8 +209,8 @@
         a, at = piece // half, pl.ds(piece % half * tall, tall)
         first, second = ((one_gate, other_gate), (one_up, other_up))[a]
         return (
-            pltpu.make_async_copy(first.at[at], ones.at[a, at], in_sem.at[piece]),
-            pltpu.make_async_copy(second.at[at], others.at[a, at], in_sem.at[piece]),
+            pltpu.make_async_copy(first.at[at], ones.at[a, at], in_sem.at[piece // group]),
+            pltpu.make_async_copy(second.at[at], others.at[a, at], in_sem.at[piece // group]),
         )
 
     for piece in range(half):
@@ -221,7 +222,8 @@
     def mix_and_sum(a):
         total = jnp.zeros((8, cols), jnp.float32)
         for piece in range(a * half, (a + 1) * half):
-            took(ones.at[:, pl.ds(0, tall)], in_sem.at[piece])
+            if piece % group == 0:
+                took(ones.at[:, pl.ds(0, group * tall)], in_sem.at[piece // group])
             if piece == half - 1:
                 for later in range(half, pieces):
                     for copy in reads(later):
@@ -518,7 +520,7 @@
             pltpu.VMEM((3, ahead, cols), jnp.float32),
             kinds.DMA((1,)),
             kinds.DMA((3,)),
-            kinds.DMA((pieces,)),
+            kinds.DMA((pieces // (2 - pieces // 2 % 2),)),
             kinds.DMA((2,)),
             kinds.DMA((1,)),
             kinds.DMA((3,)),

time: 169 us -> 169 us (level)
  no operation moved by 1% of the time
where the time goes in v8:
time: 169 us; the launch traced here: 168 us
  Pallas kernels  167 us (99%)
    pallas_call x1, Pallas kernels, shards(): pl.pallas_call(functools.partial(gather_kernel, n, parts, pieces, ahead,...  154 us
    pallas_call x1, Pallas kernels, shards(): pl.pallas_call(functools.partial(last_kernel, n, lates), out_shape=pltpu....  6.45 us
    pallas_call x1, Pallas kernels, shards(): pl.pallas_call(write_kernel, out_shape=whole + (jax.ShapeDtypeStruct((1,...  5.8 us

profile of v8, /device:TPU:0, one launch (start us, length us, event | category | flops | bytes accessed | tf_op | source)
XLA Modules:
  0.0 167.8 jit_solution(11441657097116447498)
XLA Ops:
  0.6 154.2 %mix_gather.1 = (bf16[4096,2048]{1,0:T(8,128)(2,1)S(1)}, bf16[320,2048]{1,0:T(8,128)(2,1)S(1)}, f32[1,2048]{1,0:T(1,128)S(1)}, f32[1,2048]{1,0:T(1,128)S(1)}, bf16[16,128]{1,0:T(8,128)(2,1)S(1)}) custom-call(f32[256,2048]{1,0:T(8,128)} %one_gate.1, f32[256,2048]{1,0:T(8,128)} %other_gate.1, f32[256,2048]{1,0:T(8,128)} %one_up.1, f32[256,2048]{1,0:T(8,128)} %other_up.1, ...), custom_call_target="tpu_custom_call" | custom-call | tf_op jit(solution)/shard_map/mix_gather/pallas_call | solution.py:500
  154.9 5.8 %write_out.1 = (bf16[2048,2048]{1,0:T(8,128)(2,1)}, bf16[2048,2048]{1,0:T(8,128)(2,1)}, f32[1,2048]{1,0:T(1,128)}, f32[1,2048]{1,0:T(1,128)}, bf16[16,128]{1,0:T(8,128)(2,1)}, /*index=5*/f32[8,128]{1,0:T(8,128)S(1)}) custom-call(bf16[4096,2048]{1,0:T(8,128)(2,1)S(1)} %get-tuple-element.19.held, f32[1,2048]{1,0:T(1,128)S(1)} %get-tuple-element.20.factor_gate, ...), custom_call_target="tpu_custom_call" | custom-call | tf_op jit(solution)/shard_map/write_out/pallas_call | solution.py:542
  160.7 6.4 %gather_last.1.more = bf16[2,320,2048]{2,1,0:T(8,128)(2,1)S(1)} custom-call(bf16[320,2048]{1,0:T(8,128)(2,1)S(1)} %get-tuple-element.18.left, f32[8,128]{1,0:T(8,128)S(1)} %get-tuple-element.23.token), custom_call_target="tpu_custom_call" | custom-call | tf_op jit(solution)/shard_map/gather_last/pallas_call | solution.py:552
  167.1 0.7 write_last.1
